TPU v7x, 32 devices: a whole 2x2x4 slice. The times are simulated.
32 devices in a mesh: morton: 8 (over z, x), level: 4 (over y, core).
Axes of the slice: x: 2, y: 2, z: 4, core: 2. Of those that a mesh axis runs over, the one named last changes fastest.
Arguments:
- coarse_density: float32 [4096, 128], P('morton'), may hold values from 0.000125 to 0.12
- coarse_emission: float32 [4096, 128], P('morton'), may hold values from 0 to 4
- fine_density: float32 [16384, 128], P(('morton', 'level')), may hold values from 0.000125 to 0.12
- fine_emission: float32 [16384, 128], P(('morton', 'level')), may hold values from 0 to 4
- coarse_brick: int32 [32768], P(('morton', 'level')), may hold values from 0 to 15
- coarse_lane: int32 [32768], P(('morton', 'level')), may hold values from 0 to 1023
- coarse_entry: int32 [32768], P(('morton', 'level')), may hold values from 0 to 31, as said below
- coarse_count: int32 [32768], P(('morton', 'level')), may hold values from 0 to 32, as said below
- fine_owner: int32 [262144, 1], P(('morton', 'level')), may hold values from 0 to 31; in each aligned block of 8192 rows (0 to 8191, 8192 to 16383, ...) at most 512 rows name the same one
- fine_brick: int32 [262144], P(('morton', 'level')), may hold values from 0 to 1
- fine_lane: int32 [262144], P(('morton', 'level')), may hold values from 0 to 1023
- fine_entry: int32 [262144], P(('morton', 'level')), may hold values from 0 to 31, as said below
- fine_count: int32 [262144], P(('morton', 'level')), may hold values from 0 to 32, as said below
Outputs:
- image_color: float32 [8192], P(('morton', 'level'))
- transmittance: float32 [8192], P(('morton', 'level'))
Inputs may be any that keep to these rules, and one draw needn't show every extreme that they name: `coarse_entry`: entry plus count is at most 32 for each segment. `coarse_count`: count 0 marks an empty segment. `fine_entry`: entry plus count is at most 32 for each segment. `fine_count`: count 0 marks a padded slot. `fine_owner`: among the fine segments of one device, at most 512 name one owner device, a bound that some block reaches.
All inputs are finite; a program needn't handle non-finite values.
Results may differ from a plain program's by a relative error of at most 0.0003.
Values sent between devices are 32-bit elements; how exact they have to be, the bound alone decides.
A program may use at most 64 MiB of HBM per device.

v0:
```python
import functools

import jax
import jax.numpy as jnp
from jax import lax
from jax.experimental import pallas as pl
from jax.experimental.pallas import tpu as pltpu
from jax.sharding import PartitionSpec as P

BRICK = 32
LANES = 128
PER_ROW = LANES // BRICK
BROWS = BRICK**3 // LANES
F32 = jnp.float32
BF16 = jnp.bfloat16
I32 = jnp.int32
CODE_BITS = 22
PRESENT = 1 << CODE_BITS
BLOCK = 512
VMEM = pl.BlockSpec(memory_space=pltpu.VMEM)


def onehot(ids, width):
    rows = lax.broadcasted_iota(I32, (width, ids.shape[1]), 0)
    return jnp.where(rows == ids, 1.0, 0.0).astype(F32)


def split(x, parts):
    out = []
    for _ in range(parts):
        piece = x.astype(BF16)
        out.append(piece)
        x = x - piece.astype(F32)
    return out


def dot_nt(a, b):
    return lax.dot_general(a, b, (((1,), (1,)), ((), ())), preferred_element_type=F32)


def dot_nn(a, b):
    return jnp.dot(a, b, preferred_element_type=F32)


def rank_in(ones, upper, carry):
    within = dot_nn(ones.astype(BF16), upper)
    ranks = jnp.sum((within + carry) * ones, axis=0, keepdims=True)
    return ranks, carry + jnp.sum(ones, axis=1, keepdims=True)


def place(dest_ones, codes, slots, cap):
    pieces = [codes & 255, (codes >> 8) & 255, codes >> 16]
    left = jnp.concatenate([dest_ones * piece.astype(F32) for piece in pieces], axis=0)
    return dot_nt(left.astype(BF16), onehot(slots, cap).astype(BF16))


def join(placed, n):
    a, b, c = (placed[i * n : (i + 1) * n].astype(I32) for i in range(3))
    return a + (b << 8) + (c << 16)


def paired_loop(steps, body, state):
    by = 2 if steps % 2 == 0 else 1

    def some(j, state):
        for u in range(by):
            state = body(by * j + u, state)
        return state

    return lax.fori_loop(0, steps // by, some, state)


def route(
    n_morton, n_level, cap_f, cap_c, fine_ref, coarse_ref, msg_ref, rank_ref, dest_ref, slot_ref, upper_ref
):
    n_dev = n_morton * n_level
    block = upper_ref.shape[0]
    upper_ref[...] = jnp.where(
        lax.broadcasted_iota(I32, (block, block), 0) < lax.broadcasted_iota(I32, (block, block), 1), 1.0, 0.0
    ).astype(BF16)
    depth, pixels = fine_ref.shape
    mask = PRESENT - 1

    def one_row(f, state):
        carry, placed = state
        for h in range(0, pixels, block):
            packed = fine_ref[pl.ds(f, 1), h : h + block]
            ones = onehot(packed >> CODE_BITS, n_dev)
            ranks, carry = rank_in(ones, upper_ref[...], carry)
            ranks = ranks.astype(I32)
            rank_ref[pl.ds(f, 1), h : h + block] = ranks
            placed = placed + place(ones, (packed & mask) | PRESENT, ranks, cap_f)
        return carry, placed

    state = (jnp.zeros((n_dev, 1), F32), jnp.zeros((3 * n_dev, cap_f), F32))
    _, placed = paired_loop(depth, one_row, state)
    fine_msg = join(placed, n_dev)
    carry = jnp.zeros((n_morton, 1), F32)
    placed = jnp.zeros((3 * n_dev, cap_c), F32)
    for h in range(0, pixels, block):
        packed = coarse_ref[:, h : h + block]
        group = packed >> CODE_BITS
        ranks, carry = rank_in(onehot(group, n_morton), upper_ref[...], carry)
        slots = jnp.floor((ranks + 0.5) * (1.0 / n_level)).astype(I32)
        dest = group * n_level + (ranks.astype(I32) - slots * n_level)
        dest_ref[:, h : h + block] = dest
        slot_ref[:, h : h + block] = slots
        placed = placed + place(onehot(dest, n_dev), (packed & mask) | PRESENT, slots, cap_c)
    coarse_msg = join(placed, n_dev)
    for i in range(n_dev):
        msg_ref[i, :, :cap_f] = fine_msg[i : i + 1]
        msg_ref[i, :, cap_f:] = coarse_msg[i : i + 1]


def cells_of(shape):
    rows = lax.broadcasted_iota(I32, shape, 0)
    return (rows & -BRICK) + 4 * (rows & 7) + ((rows >> 3) & 3)


def turn_tables(pairs):
    turn = jnp.where(
        cells_of((LANES, LANES)) == lax.broadcasted_iota(I32, (LANES, LANES), 1), 1.0, 0.0
    ).astype(BF16)
    for table_ref, dens_ref, emis_ref in pairs:
        for at, ref in ((0, dens_ref), (LANES, emis_ref)):
            for i, piece in enumerate(split(ref[...], 2)):
                top = 2 * LANES * i + at
                table_ref[top : top + LANES, :] = dot_nt(turn, piece).astype(BF16)


def fetch(codes, table_ref, got_ref):
    ones = onehot((codes & (PRESENT - 1)) >> 13, table_ref.shape[1]).astype(BF16)
    both = dot_nn(table_ref[...], ones)
    got_ref[...] = both[: 2 * LANES] + both[2 * LANES :]


def march(codes, got_ref, at):
    step = LANES
    first = (codes >> 6) & 127
    last = first + (codes & 63)
    cells = cells_of((LANES, step))
    inside = (cells >= first) & (cells < last)
    dens = jnp.where(inside, got_ref[:LANES, at : at + step], 0.0)
    emis = jnp.where(inside, got_ref[LANES:, at : at + step], 0.0)
    dens = sum(dens[g * BRICK : (g + 1) * BRICK] for g in range(PER_ROW))
    emis = sum(emis[g * BRICK : (g + 1) * BRICK] for g in range(PER_ROW))
    trans = jnp.exp(-dens)
    color = (1.0 - trans) * emis
    c, t = color[24:32], trans[24:32]
    for k in (2, 1, 0):
        tk = trans[8 * k : 8 * k + 8]
        c = color[8 * k : 8 * k + 8] + tk * c
        t = tk * t
    for shift in (1, 2, 4):
        c = c + t * pltpu.roll(c, 8 - shift, 0)
        t = t * pltpu.roll(t, 8 - shift, 0)
    return c[0:1], t[0:1]


def frame_kernel(
    n_morton,
    n_level,
    cap_f,
    cap_c,
    fine_ref,
    coarse_ref,
    *refs,
):
    tables, (out_ref, *refs) = refs[:4], refs[4:]
    (
    rank_ref,
    dest_ref,
    slot_ref,
    upper_ref,
    ft_ref,
    ct_ref,
    fl_ref,
    cl_ref,
    msg_ref,
    code_ref,
    served_ref,
    resp_ref,
    slab_ref,
    ask_send,
    ask_recv,
    tell_send,
    tell_recv,
    join_send,
    join_recv,
    table_sems,
    *refs,
    ) = refs
    copies = [
        pltpu.make_async_copy(src, dst, table_sems.at[i]) for i, (src, dst) in enumerate(zip(tables, refs[:4]))
    ]
    fd_ref, fe_ref, cd_ref, ce_ref = refs[:4]
    got_refs = refs[4:]
    for copy in copies:
        copy.start()
    n_dev = n_morton * n_level
    level = lax.axis_index("level")
    me = lax.axis_index("morton") * n_level + level
    mesh_ids = pl.DeviceIdType.MESH

    def device(d):
        return d // n_level, lax.rem(d, n_level)

    def after(k):
        return lax.rem(me + k, n_dev)

    def before(k):
        return lax.rem(me + n_dev - k, n_dev)

    def ask(k):
        to = after(k)
        return pltpu.make_async_remote_copy(
            src_ref=msg_ref.at[to],
            dst_ref=code_ref.at[me],
            send_sem=ask_send.at[k],
            recv_sem=ask_recv.at[k],
            device_id=device(to),
            device_id_type=mesh_ids,
        )

    def tell(k):
        to = before(k)
        return pltpu.make_async_remote_copy(
            src_ref=served_ref.at[to],
            dst_ref=resp_ref.at[me],
            send_sem=tell_send.at[k],
            recv_sem=tell_recv.at[k],
            device_id=device(to),
            device_id_type=mesh_ids,
        )

    def join(k):
        to = lax.rem(level + k, n_level)
        return pltpu.make_async_remote_copy(
            src_ref=slab_ref.at[to],
            dst_ref=out_ref.at[level],
            send_sem=join_send.at[k],
            recv_sem=join_recv.at[k],
            device_id=(lax.axis_index("morton"), to),
            device_id_type=mesh_ids,
        )

    barrier = pltpu.get_barrier_semaphore()

    def each(low, high, act):
        def body(k, _):
            act(k)
            return 0

        lax.fori_loop(low, high, body, 0)

    each(1, n_dev, lambda k: pl.semaphore_signal(barrier, inc=1, device_id=device(after(k)), device_id_type=mesh_ids))
    route(
        n_morton, n_level, cap_f, cap_c, fine_ref, coarse_ref, msg_ref, rank_ref, dest_ref, slot_ref, upper_ref
    )
    pl.semaphore_wait(barrier, n_dev - 1)
    each(1, n_dev, lambda k: ask(k).start())
    code_ref[me] = msg_ref[me]
    for copy in copies:
        copy.wait()
    turn_tables(((ft_ref, fd_ref, fe_ref), (ct_ref, cd_ref, ce_ref)))
    def put(i, at, c, t):
        served_ref[i, 0:1, at : at + LANES] = c
        served_ref[i, 1:2, at : at + LANES] = t

    def fetch_source(i, bufs):
        fetch(code_ref[i, :, :cap_f], ft_ref, bufs[0])
        fetch(code_ref[i, :, cap_f:], ct_ref, bufs[1])

    def march_source(i, bufs):
        for at in range(0, cap_f, LANES):
            put(i, at, *march(code_ref[i, :, at : at + LANES], bufs[0], at))
        for at in range(0, cap_c, LANES):
            put(i, cap_f + at, *march(code_ref[i, :, cap_f + at : cap_f + at + LANES], bufs[1], at))

    even, odd = got_refs[:2], got_refs[2:]
    for ref in odd:
        ref[...] = jnp.zeros(ref.shape, F32)

    def two_sources(j, _):
        for u in range(2):

            @pl.when(2 * j + u > 0)
            def _():
                ask(2 * j + u).wait_recv()

            @pl.when(2 * j - 3 + u > 0)
            def _():
                tell(2 * j - 3 + u).start()

        now, later = before(2 * j), before(2 * j + 1)
        fetch_source(now, even)
        march_source(before(jnp.maximum(2 * j - 1, 0)), odd)
        fetch_source(later, odd)
        march_source(now, even)
        return 0

    lax.fori_loop(0, n_dev // 2, two_sources, 0)
    for k in (n_dev - 3, n_dev - 2):
        if k > 0:
            tell(k).start()
    march_source(before(n_dev - 1), odd)
    tell(n_dev - 1).start()
    resp_ref[me] = served_ref[me]
    each(1, n_dev, lambda k: tell(k).wait_recv())
    blend(cap_f, resp_ref, fine_ref, rank_ref, dest_ref, slot_ref, slab_ref, fl_ref, cl_ref)
    for k in range(1, n_level):
        join(k).start()
    out_ref[level] = slab_ref[level]
    each(1, n_dev, lambda k: ask(k).wait_send())
    each(1, n_dev, lambda k: tell(k).wait_send())
    for k in range(1, n_level):
        join(k).wait()


def look_up(left, ones, dest_ones, n):
    got = dot_nn(left, ones)
    vals = []
    for v in range(2):
        total = sum(got[(v * 3 + i) * n : (v * 3 + i + 1) * n] for i in range(3))
        vals.append(jnp.sum(total * dest_ones, axis=0, keepdims=True))
    return vals


def blend(cap_f, resp_ref, fine_ref, rank_ref, dest_ref, slot_ref, out_ref, fl_ref, cl_ref):
    n_dev, _, cap = resp_ref.shape
    depth, pixels = fine_ref.shape
    for v in range(2):
        full = resp_ref[:, v, :]
        for i, piece in enumerate(split(full, 3)):
            at = (v * 3 + i) * n_dev
            fl_ref[at : at + n_dev, :] = piece[:, :cap_f]
            cl_ref[at : at + n_dev, :] = piece[:, cap_f:]
    block = min(BLOCK, pixels)
    for h in range(0, pixels, block):
        c, t = look_up(
            cl_ref[...],
            onehot(slot_ref[:, h : h + block], cap - cap_f).astype(BF16),
            onehot(dest_ref[:, h : h + block], n_dev),
            n_dev,
        )

        def one_row(f, state):
            c, t = state
            fc, ft = look_up(
                fl_ref[...],
                onehot(rank_ref[pl.ds(f, 1), h : h + block], cap_f).astype(BF16),
                onehot(fine_ref[pl.ds(f, 1), h : h + block] >> CODE_BITS, n_dev),
                n_dev,
            )
            return c + t * fc, t * ft

        c, t = paired_loop(depth, one_row, (c, t))
        quarter = out_ref.shape[2]
        for at in range(0, block, quarter):
            part = (h + at) // quarter
            out_ref[part, 0:1, :] = c[:, at : at + quarter]
            out_ref[part, 1:2, :] = t[:, at : at + quarter]


def shards(
    coarse_density,
    coarse_emission,
    fine_density,
    fine_emission,
    coarse_brick,
    coarse_lane,
    coarse_entry,
    coarse_count,
    fine_owner,
    fine_brick,
    fine_lane,
    fine_entry,
    fine_count,
):
    n_morton = lax.axis_size("morton")
    n_level = lax.axis_size("level")
    n_dev = n_morton * n_level
    segments = fine_brick.shape[0]
    pixels = coarse_brick.shape[0]
    per_pixel = segments // pixels
    cap_f = -(-(2 * segments // n_dev) // LANES) * LANES
    cap_c = -(-pixels // (n_level * LANES)) * LANES
    cap = cap_f + cap_c
    c_rows = coarse_density.shape[0]
    block = min(BLOCK, pixels)

    def pack(owner, row, lane, entry, count):
        code = (((row * PER_ROW + lane % PER_ROW) * BRICK + entry) << 6) + count
        return (owner << CODE_BITS) | code

    fine = pack(
        fine_owner[:, 0], fine_brick * BROWS + fine_lane // PER_ROW, fine_lane, fine_entry, fine_count
    )
    fine = fine.reshape(pixels, per_pixel).T
    row = coarse_brick * BROWS + coarse_lane // PER_ROW
    coarse = pack(row // c_rows, row % c_rows, coarse_lane, coarse_entry, coarse_count).reshape(1, pixels)
    quarter = pixels // n_level
    rows = fine_density.shape[0]
    sems = [pltpu.SemaphoreType.DMA((n_dev,))] * 4 + [pltpu.SemaphoreType.DMA((n_level,))] * 2
    parts = pl.pallas_call(
        functools.partial(frame_kernel, n_morton, n_level, cap_f, cap_c),
        out_shape=jax.ShapeDtypeStruct((n_level, 2, quarter), F32),
        in_specs=[VMEM] * 2 + [pl.BlockSpec(memory_space=pl.ANY)] * 4,
        out_specs=VMEM,
        scratch_shapes=[
            pltpu.VMEM((per_pixel, pixels), I32),
            pltpu.VMEM((1, pixels), I32),
            pltpu.VMEM((1, pixels), I32),
            pltpu.VMEM((block, block), BF16),
            pltpu.VMEM((4 * LANES, rows), BF16),
            pltpu.VMEM((4 * LANES, c_rows), BF16),
            pltpu.VMEM((6 * n_dev, cap_f), BF16),
            pltpu.VMEM((6 * n_dev, cap_c), BF16),
            pltpu.VMEM((n_dev, 1, cap), I32),
            pltpu.VMEM((n_dev, 1, cap), I32),
            pltpu.VMEM((n_dev, 2, cap), F32),
            pltpu.VMEM((n_dev, 2, cap), F32),
            pltpu.VMEM((n_level, 2, quarter), F32),
        ]
        + sems
        + [pltpu.SemaphoreType.DMA((4,))]
        + [pltpu.VMEM((rows, LANES), F32)] * 2
        + [pltpu.VMEM((c_rows, LANES), F32)] * 2
        + [pltpu.VMEM((2 * LANES, cap_f), F32), pltpu.VMEM((2 * LANES, cap_c), F32)] * 2,
        compiler_params=pltpu.CompilerParams(collective_id=0, has_side_effects=True),
    )(fine, coarse, fine_density, fine_emission, coarse_density, coarse_emission)
    color, trans = parts[0, 0], parts[0, 1]
    for s in range(1, n_level):
        color = color + trans * parts[s, 0]
        trans = trans * parts[s, 1]
    return color, trans


def solution(mesh):
    both = P(("morton", "level"))
    rows = P(("morton", "level"), None)
    coarse = P("morton", None)
    return jax.shard_map(
        shards,
        mesh=mesh,
        in_specs=(coarse, coarse, rows, rows, both, both, both, both, rows, both, both, both, both),
        out_specs=(both, both),
        check_vma=False,
    )
```

profile of v0, /device:TPU:0, one launch (start us, length us, event | category | flops | bytes accessed | tf_op | source)
XLA Modules:
  0.0 51.7 jit_solution(11642807274762538885)
XLA Ops:
  0.6 0.0 copy-start.1
  0.6 0.0 copy-start
  0.7 0.8 %broadcast_shift-left_fusion = s32[8192,1]{0,1:T(1,128)S(1)} fusion(s32[8192,1]{0,1:T(1,128)} %param.21), kind=kLoop, calls=%fused_computation.18 | loop fusion | flops 8192 | bytes 65536 | tf_op jit(solution)/shard_map/shift_left | solution.py:394
  1.5 0.0 copy-done.1
  1.5 0.0 copy-done
  1.5 0.8 %fusion.7 = s32[8192]{0:T(1024)S(1)} fusion(s32[8192]{0:T(1024)S(1)} %bitcast.6, s32[8192]{0:T(1024)S(1)} %copy-done, s32[8192]{0:T(1024)S(1)} %copy-done.1, s32[8192]{0:T(1024)} %param.22, s32[8192]{0:T(1024)} %param.23), kind=kLoop, calls=%fused_computation.12 | loop fusion | flops 229376 | bytes 196608 | tf_op jit(solution)/shard_map/or | solution.py:394
  2.3 0.3 reshape.21
  2.6 0.0 copy-start.2
  2.6 0.0 copy-start.3
  2.6 0.0 copy-start.4
  2.6 0.0 copy-start.5
  2.6 0.8 %copy.15 = s32[1024,8]{0,1:T(8,128)} copy(s32[1024,8]{1,0:T(8,128)S(1)} %reshape.21) | data formatting | bytes 65536 | tf_op jit(solution)/shard_map/reshape | solution.py:399
  3.4 0.0 copy-done.2
  3.4 0.0 copy-done.3
  3.4 0.0 copy-done.4
  3.4 0.0 copy-done.5
  3.4 0.6 %fusion.14 = s32[1024]{0:T(1024)} fusion(s32[1024]{0:T(1024)S(1)} %copy-done.2, s32[1024]{0:T(1024)S(1)} %copy-done.3, s32[1024]{0:T(1024)S(1)} %copy-done.4, s32[1024]{0:T(1024)S(1)} %copy-done.5), kind=kLoop, calls=%fused_computation.31 | loop fusion | flops 49152 | bytes 20480 | tf_op jit(solution)/shard_map/or | solution.py:394
  4.1 46.3 %shard_map.140 = f32[4,2,256]{2,1,0:T(2,128)} custom-call(s32[8,1024]{1,0:T(8,128)} %bitcast.5, s32[1,1024]{1,0:T(1,128)} %bitcast.7, f32[512,128]{1,0:T(8,128)} %refs_0_.1, f32[512,128]{1,0:T(8,128)} %refs_1_.1, f32[512,128]{1,0:T(8,128)} %refs_2_.1, f32[512,128]{1,0:T(8,128)} %refs_3_.1), custom_call_target="tpu_custom_call" | custom-call | tf_op jit(solution)/shard_map/pallas_call | solution.py:405
  50.4 1.3 %slice_multiply_fusion = (f32[1,1,256]{2,1,0:T(1,128)}, f32[1,1,256]{2,1,0:T(1,128)}) fusion(f32[4,2,256]{2,1,0:T(2,128)} %shard_map.140), kind=kLoop, calls=%fused_computation.46 | loop fusion | flops 2304 | bytes 10240 | tf_op jit(solution)/shard_map/mul | solution.py:435
Async XLA Ops:
  0.6 0.8 %copy-start.1 = (s32[8192]{0:T(1024)S(1)}, s32[8192]{0:T(1024)}, u32[]{:S(2)}) copy-start(s32[8192]{0:T(1024)} %param.24) | copy-start | bytes 98308
  0.6 0.8 %copy-start = (s32[8192]{0:T(1024)S(1)}, s32[8192]{0:T(1024)}, u32[]{:S(2)}) copy-start(s32[8192]{0:T(1024)} %param.25) | copy-start | bytes 98308
  2.6 0.8 %copy-start.2 = (s32[1024]{0:T(1024)S(1)}, s32[1024]{0:T(1024)}, u32[]{:S(2)}) copy-start(s32[1024]{0:T(1024)} %param.20) | copy-start | bytes 12292
  2.6 0.8 %copy-start.3 = (s32[1024]{0:T(1024)S(1)}, s32[1024]{0:T(1024)}, u32[]{:S(2)}) copy-start(s32[1024]{0:T(1024)} %param.19) | copy-start | bytes 12292
  2.6 0.8 %copy-start.4 = (s32[1024]{0:T(1024)S(1)}, s32[1024]{0:T(1024)}, u32[]{:S(2)}) copy-start(s32[1024]{0:T(1024)} %param.18) | copy-start | bytes 12292
  2.6 0.8 %copy-start.5 = (s32[1024]{0:T(1024)S(1)}, s32[1024]{0:T(1024)}, u32[]{:S(2)}) copy-start(s32[1024]{0:T(1024)} %param.17) | copy-start | bytes 12292
where the time goes:
time: 52.1 us; the launch traced here: 51.7 us
  Pallas kernels  46.3 us (89%)
  other arithmetic  3.58 us (7%)
  local copies, waits for them, and re-layouts  1.11 us (2%)
  between operations  0.72 us (1%)
    pallas_call x1, Pallas kernels, shards(): pl.pallas_call(functools.partial(frame_kernel, n_morton, n_level, cap_f,...  46.3 us
    or x2, other arithmetic, pack(): return owner << CODE_BITS | code  1.44 us
    mul x1, other arithmetic, shards(): trans = trans * parts[s, 1]  1.35 us
    reshape x2, local copies, waits for them, and re-layouts, shards(): fine = fine.reshape(pixels, per_pixel).T  1.07 us

commit v1 on v0

v1 whole, which is shorter than its diff:
```python
import functools

import jax
import jax.numpy as jnp
from jax import lax
from jax.experimental import pallas as pl
from jax.experimental.pallas import tpu as pltpu
from jax.sharding import PartitionSpec as P

BRICK = 32
LANES = 128
SUBS = 8
PER_ROW = LANES // BRICK
COLUMNS = BRICK**2
F32 = jnp.float32
BF16 = jnp.bfloat16
I32 = jnp.int32
VMEM = pl.BlockSpec(memory_space=pltpu.VMEM)
ANY = pl.BlockSpec(memory_space=pl.ANY)


def iota(shape, dim):
    return lax.broadcasted_iota(I32, shape, dim)


def onehot(ids, width):
    return jnp.where(iota((width, ids.shape[1]), 0) == ids, 1.0, 0.0).astype(F32)


def split(x, parts):
    out = []
    for _ in range(parts):
        piece = x.astype(BF16)
        out.append(piece)
        x = x - piece.astype(F32)
    return out


def dot_nt(a, b):
    return lax.dot_general(a, b, (((1,), (1,)), ((), ())), preferred_element_type=F32)


def dot_nn(a, b):
    return jnp.dot(a, b, preferred_element_type=F32)


def across(ref, at, rows):
    return jnp.concatenate([ref[at + r : at + r + 1, :] for r in range(rows)], axis=1)


def rank_rows(ids_ref, width, ones_ref, within_ref, out_ref):
    rows = ids_ref.shape[0]
    for r in range(rows):
        ones_ref[r * width : (r + 1) * width, :] = onehot(ids_ref[r : r + 1, :], width).astype(BF16)
    lane, other = iota((LANES, 2 * LANES), 0), iota((LANES, 2 * LANES), 1)
    counter = jnp.where((lane < other) | (other >= LANES), 1.0, 0.0).astype(BF16)
    used = rows * width
    within_ref[:used, :] = dot_nn(ones_ref[:used, :], counter)
    ids_of = iota((width, LANES), 0)
    carry = jnp.zeros((width, LANES), F32)
    for r in range(rows):
        part = within_ref[r * width : (r + 1) * width, :]
        mine = jnp.where(ids_of == ids_ref[r : r + 1, :], part[:, :LANES] + carry, 0.0)
        out_ref[r : r + 1, :] = jnp.sum(mine, axis=0, keepdims=True).astype(I32)
        carry = carry + part[:, LANES:]


def place(cell_ref, lane_ref, code_ref, cells, chunk):
    rows = cell_ref.shape[0]
    placed = jnp.zeros((3 * cells, LANES), F32)
    for r in range(0, rows, chunk):
        here = iota((cells, chunk * LANES), 0) == across(cell_ref, r, chunk)
        code = across(code_ref, r, chunk)
        pieces = [code & 255, (code >> 8) & 255, code >> 16]
        left = jnp.concatenate([jnp.where(here, p.astype(F32), 0.0).astype(BF16) for p in pieces], axis=0)
        right = onehot(across(lane_ref, r, chunk), LANES).astype(BF16)
        placed = placed + dot_nt(left, right)
    a, b, c = (placed[i * cells : (i + 1) * cells].astype(I32) for i in range(3))
    return a + (b << 8) + (c << 16)


def cells_of(shape):
    rows = iota(shape, 0)
    return (rows & -BRICK) + 4 * (rows & 7) + ((rows >> 3) & 3)


def turn_tables(pairs):
    turn = jnp.where(cells_of((LANES, LANES)) == iota((LANES, LANES), 1), 1.0, 0.0).astype(BF16)
    for table_ref, dens_ref, emis_ref in pairs:
        for at, ref in ((0, dens_ref), (LANES, emis_ref)):
            for i, piece in enumerate(split(ref[...], 2)):
                top = 2 * LANES * i + at
                table_ref[top : top + LANES, :] = dot_nt(turn, piece).astype(BF16)


def fetch(codes, table_ref, got_ref):
    ones = onehot(codes >> 13, table_ref.shape[1]).astype(BF16)
    both = dot_nn(table_ref[...], ones)
    got_ref[...] = both[: 2 * LANES] + both[2 * LANES :]


def march(codes, got_ref, at):
    first = (codes >> 6) & 127
    last = first + (codes & 63)
    cells = cells_of((LANES, LANES))
    inside = (cells >= first) & (cells < last)
    dens = jnp.where(inside, got_ref[:LANES, at : at + LANES], 0.0)
    emis = jnp.where(inside, got_ref[LANES:, at : at + LANES], 0.0)
    dens = sum(dens[g * BRICK : (g + 1) * BRICK] for g in range(PER_ROW))
    emis = sum(emis[g * BRICK : (g + 1) * BRICK] for g in range(PER_ROW))
    trans = jnp.exp(-dens)
    color = (1.0 - trans) * emis
    c, t = color[24:32], trans[24:32]
    for k in (2, 1, 0):
        tk = trans[8 * k : 8 * k + 8]
        c = color[8 * k : 8 * k + 8] + tk * c
        t = tk * t
    for shift in (1, 2, 4):
        c = c + t * pltpu.roll(c, 8 - shift, 0)
        t = t * pltpu.roll(t, 8 - shift, 0)
    return c[0:1], t[0:1]


def look_up(resp_ref, at, blocks, width, cell_ref, lane_ref, left_ref, out_refs):
    n_dev, half = resp_ref.shape[0], resp_ref.shape[1] // 2
    high = blocks // width
    cells = high * n_dev
    for v in range(2):
        for h in range(high):
            for w in range(width):
                full = resp_ref[:, v * half + at + h * width + w, :]
                for i, piece in enumerate(split(full, 2)):
                    top = (2 * v + i) * cells + h * n_dev
                    left_ref[top : top + n_dev, w * LANES : (w + 1) * LANES] = piece
    rows = cell_ref.shape[0]
    chunk = SUBS
    left = left_ref[: 4 * cells, : width * LANES]
    for r in range(0, rows, chunk):
        got = dot_nn(left, onehot(across(lane_ref, r, chunk), width * LANES).astype(BF16))
        here = iota((cells, chunk * LANES), 0) == across(cell_ref, r, chunk)
        for v in range(2):
            total = got[2 * v * cells : (2 * v + 1) * cells] + got[(2 * v + 1) * cells : (2 * v + 2) * cells]
            value = jnp.sum(jnp.where(here, total, 0.0), axis=0, keepdims=True)
            for j in range(chunk):
                out_refs[v][r + j : r + j + 1, :] = value[:, j * LANES : (j + 1) * LANES]


def lanes_at(x, lanes):
    return jnp.take_along_axis(x, lanes, axis=1)


def blend(per_pixel, fine_c, fine_t, coarse_c, coarse_t, slab_ref):
    rows = fine_c.shape[0]
    level_rows = slab_ref.shape[1] // 2
    pixel_lanes = LANES // per_pixel
    lane = iota((SUBS, LANES), 1)
    source = (lane & (pixel_lanes - 1)) * per_pixel
    group = lane // pixel_lanes
    for r in range(0, rows, SUBS):
        c, t = fine_c[r : r + SUBS, :], fine_t[r : r + SUBS, :]
        shift = 1
        while shift < per_pixel:
            c = c + t * pltpu.roll(c, LANES - shift, 1)
            t = t * pltpu.roll(t, LANES - shift, 1)
            shift *= 2
        c, t = lanes_at(c, source), lanes_at(t, source)
        c, t = jnp.take_along_axis(c, group, axis=0)[0:1], jnp.take_along_axis(t, group, axis=0)[0:1]
        row = r // SUBS
        c0, t0 = coarse_c[row : row + 1, :], coarse_t[row : row + 1, :]
        to, at = row // level_rows, row % level_rows
        slab_ref[to, at : at + 1, :] = c0 + t0 * c
        slab_ref[to, level_rows + at : level_rows + at + 1, :] = t0 * t


def frame_kernel(n_morton, n_level, cap_f, cap_c, *refs):
    ints, tables, (color_ref, trans_ref), refs = refs[:9], refs[9:13], refs[13:15], refs[15:]
    int_refs, table_refs, refs = refs[:9], refs[9:13], refs[13:]
    (
        owner_ref,
        fcode_ref,
        frank_ref,
        fcell_ref,
        flane_ref,
        group_ref,
        ccode_ref,
        crank_ref,
        ccell_ref,
        clane_ref,
        ones_ref,
        within_ref,
        ft_ref,
        ct_ref,
        left_ref,
        fc_ref,
        ftr_ref,
        cc_ref,
        ctr_ref,
        msg_ref,
        code_ref,
        served_ref,
        resp_ref,
        slab_ref,
        slabs_ref,
        ask_send,
        ask_recv,
        tell_send,
        tell_recv,
        join_send,
        join_recv,
        in_sems,
        *refs,
    ) = refs
    even, odd = refs[:2], refs[2:]
    n_dev = n_morton * n_level
    nf, nc = cap_f // LANES, cap_c // LANES
    blocks = nf + nc
    copies = [
        pltpu.make_async_copy(src, dst, in_sems.at[i])
        for i, (src, dst) in enumerate(zip(ints + tables, int_refs + table_refs))
    ]
    for copy in copies[:9]:
        copy.start()
    morton, level = lax.axis_index("morton"), lax.axis_index("level")
    me = morton * n_level + level
    mesh_ids = pl.DeviceIdType.MESH

    def device(d):
        return d // n_level, lax.rem(d, n_level)

    def after(k):
        return lax.rem(me + k, n_dev)

    def before(k):
        return lax.rem(me + n_dev - k, n_dev)

    def ask(k):
        to = after(k)
        return pltpu.make_async_remote_copy(
            src_ref=msg_ref.at[to],
            dst_ref=code_ref.at[me],
            send_sem=ask_send.at[k],
            recv_sem=ask_recv.at[k],
            device_id=device(to),
            device_id_type=mesh_ids,
        )

    def tell(k):
        to = before(k)
        return pltpu.make_async_remote_copy(
            src_ref=served_ref.at[to],
            dst_ref=resp_ref.at[me],
            send_sem=tell_send.at[k],
            recv_sem=tell_recv.at[k],
            device_id=device(to),
            device_id_type=mesh_ids,
        )

    def join(k):
        to = lax.rem(level + k, n_level)
        return pltpu.make_async_remote_copy(
            src_ref=slab_ref.at[to],
            dst_ref=slabs_ref.at[level],
            send_sem=join_send.at[k],
            recv_sem=join_recv.at[k],
            device_id=(morton, to),
            device_id_type=mesh_ids,
        )

    barrier = pltpu.get_barrier_semaphore()

    def each(low, high, act):
        def body(k, _):
            act(k)
            return 0

        lax.fori_loop(low, high, body, 0)

    each(1, n_dev, lambda k: pl.semaphore_signal(barrier, inc=1, device_id=device(after(k)), device_id_type=mesh_ids))
    for copy in copies[9:]:
        copy.start()
    for copy in copies[:9]:
        copy.wait()
    f_owner, f_brick, f_lane, f_entry, f_count, c_brick, c_lane, c_entry, c_count = int_refs

    owner_ref[...] = f_owner[...]
    fcode_ref[...] = (((f_brick[...] * COLUMNS + f_lane[...]) * BRICK + f_entry[...]) << 6) + f_count[...]
    rank_rows(owner_ref, n_dev, ones_ref, within_ref, frank_ref)
    rank = frank_ref[...]
    fcell_ref[...] = f_owner[...] * nf + rank // LANES
    flane_ref[...] = rank & (LANES - 1)
    fine_msg = place(fcell_ref, flane_ref, fcode_ref, n_dev * nf, SUBS)

    c_cols = table_refs[2].shape[0] * PER_ROW
    column = c_brick[...] * COLUMNS + c_lane[...]
    group_ref[...] = column // c_cols
    ccode_ref[...] = (((column & (c_cols - 1)) * BRICK + c_entry[...]) << 6) + c_count[...]
    rank_rows(group_ref, n_morton, ones_ref, within_ref, crank_ref)
    rank = crank_ref[...]
    slot = rank // n_level
    dest = group_ref[...] * n_level + (rank & (n_level - 1))
    ccell_ref[...] = dest * nc + slot // LANES
    clane_ref[...] = slot & (LANES - 1)
    coarse_msg = place(ccell_ref, clane_ref, ccode_ref, n_dev * nc, SUBS)
    for i in range(n_dev):
        msg_ref[i, :nf, :] = fine_msg[i * nf : (i + 1) * nf]
        msg_ref[i, nf:, :] = coarse_msg[i * nc : (i + 1) * nc]

    pl.semaphore_wait(barrier, n_dev - 1)
    each(1, n_dev, lambda k: ask(k).start())
    code_ref[me] = msg_ref[me]
    for copy in copies[9:]:
        copy.wait()
    fd_ref, fe_ref, cd_ref, ce_ref = table_refs
    turn_tables(((ft_ref, fd_ref, fe_ref), (ct_ref, cd_ref, ce_ref)))

    def codes_of(i, at, rows):
        return jnp.concatenate([code_ref[i, at + r : at + r + 1, :] for r in range(rows)], axis=1)

    def fetch_source(i, bufs):
        fetch(codes_of(i, 0, nf), ft_ref, bufs[0])
        fetch(codes_of(i, nf, nc), ct_ref, bufs[1])

    def march_source(i, bufs):
        for b in range(blocks):
            buf, at = (bufs[0], b) if b < nf else (bufs[1], b - nf)
            c, t = march(code_ref[i, b : b + 1, :], buf, at * LANES)
            served_ref[i, b : b + 1, :] = c
            served_ref[i, blocks + b : blocks + b + 1, :] = t

    for ref in odd:
        ref[...] = jnp.zeros(ref.shape, F32)

    def two_sources(j, _):
        for u in range(2):

            @pl.when(2 * j + u > 0)
            def _():
                ask(2 * j + u).wait_recv()

            @pl.when(2 * j - 3 + u > 0)
            def _():
                tell(2 * j - 3 + u).start()

        now, later = before(2 * j), before(2 * j + 1)
        fetch_source(now, even)
        march_source(before(jnp.maximum(2 * j - 1, 0)), odd)
        fetch_source(later, odd)
        march_source(now, even)
        return 0

    lax.fori_loop(0, n_dev // 2, two_sources, 0)
    for k in (n_dev - 3, n_dev - 2):
        if k > 0:
            tell(k).start()
    march_source(before(n_dev - 1), odd)
    tell(n_dev - 1).start()
    resp_ref[me] = served_ref[me]
    rank = frank_ref[...]
    wf, wc = min(nf, 2), min(nc, 2)
    fcell_ref[...] = owner_ref[...] + (rank // (wf * LANES)) * n_dev
    flane_ref[...] = rank & (wf * LANES - 1)
    rank = crank_ref[...]
    slot = rank // n_level
    ccell_ref[...] = group_ref[...] * n_level + (rank & (n_level - 1)) + (slot // (wc * LANES)) * n_dev
    clane_ref[...] = slot & (wc * LANES - 1)
    each(1, n_dev, lambda k: tell(k).wait_recv())
    look_up(resp_ref, nf, nc, wc, ccell_ref, clane_ref, left_ref, (cc_ref, ctr_ref))
    look_up(resp_ref, 0, nf, wf, fcell_ref, flane_ref, left_ref, (fc_ref, ftr_ref))
    blend(owner_ref.shape[0] // group_ref.shape[0], fc_ref, ftr_ref, cc_ref, ctr_ref, slab_ref)
    for k in range(1, n_level):
        join(k).start()
    slabs_ref[level] = slab_ref[level]
    each(1, n_dev, lambda k: ask(k).wait_send())
    each(1, n_dev, lambda k: tell(k).wait_send())
    for k in range(1, n_level):
        join(k).wait()
    rows = color_ref.shape[0]
    color, trans = slabs_ref[0, :rows, :], slabs_ref[0, rows:, :]
    for s in range(1, n_level):
        color = color + trans * slabs_ref[s, :rows, :]
        trans = trans * slabs_ref[s, rows:, :]
    color_ref[...] = color
    trans_ref[...] = trans


def shards(
    coarse_density,
    coarse_emission,
    fine_density,
    fine_emission,
    coarse_brick,
    coarse_lane,
    coarse_entry,
    coarse_count,
    fine_owner,
    fine_brick,
    fine_lane,
    fine_entry,
    fine_count,
):
    n_morton = lax.axis_size("morton")
    n_level = lax.axis_size("level")
    n_dev = n_morton * n_level
    segments = fine_brick.shape[0]
    pixels = coarse_brick.shape[0]
    cap_f = -(-(2 * segments // n_dev) // LANES) * LANES
    cap_c = -(-pixels // (n_level * LANES)) * LANES
    nf, nc = cap_f // LANES, cap_c // LANES
    blocks = nf + nc
    f_rows, c_rows = segments // LANES, pixels // LANES
    level_rows = c_rows // n_level
    ints = [x.reshape(f_rows, LANES) for x in (fine_owner, fine_brick, fine_lane, fine_entry, fine_count)]
    ints += [x.reshape(c_rows, LANES) for x in (coarse_brick, coarse_lane, coarse_entry, coarse_count)]
    tables = [fine_density, fine_emission, coarse_density, coarse_emission]
    t_rows, g_rows = fine_density.shape[0], coarse_density.shape[0]
    wide = max(f_rows * n_dev, c_rows * n_morton)
    left_rows = 4 * n_dev * max(nf // min(nf, 2), nc // min(nc, 2))

    def like(x):
        return pltpu.VMEM(x.shape, x.dtype)

    sems = [pltpu.SemaphoreType.DMA((n_dev,))] * 4 + [pltpu.SemaphoreType.DMA((n_level,))] * 2
    color, trans = pl.pallas_call(
        functools.partial(frame_kernel, n_morton, n_level, cap_f, cap_c),
        out_shape=[jax.ShapeDtypeStruct((level_rows, LANES), F32)] * 2,
        in_specs=[ANY] * 13,
        out_specs=[VMEM] * 2,
        scratch_shapes=[like(x) for x in ints + tables]
        + [pltpu.VMEM((f_rows, LANES), I32)] * 5
        + [pltpu.VMEM((c_rows, LANES), I32)] * 5
        + [
            pltpu.VMEM((wide, LANES), BF16),
            pltpu.VMEM((wide, 2 * LANES), F32),
            pltpu.VMEM((4 * LANES, t_rows), BF16),
            pltpu.VMEM((4 * LANES, g_rows), BF16),
            pltpu.VMEM((left_rows, 2 * LANES), BF16),
        ]
        + [pltpu.VMEM((f_rows, LANES), F32)] * 2
        + [pltpu.VMEM((c_rows, LANES), F32)] * 2
        + [
            pltpu.VMEM((n_dev, blocks, LANES), I32),
            pltpu.VMEM((n_dev, blocks, LANES), I32),
            pltpu.VMEM((n_dev, 2 * blocks, LANES), F32),
            pltpu.VMEM((n_dev, 2 * blocks, LANES), F32),
            pltpu.VMEM((n_level, 2 * level_rows, LANES), F32),
            pltpu.VMEM((n_level, 2 * level_rows, LANES), F32),
        ]
        + sems
        + [pltpu.SemaphoreType.DMA((13,))]
        + [pltpu.VMEM((2 * LANES, cap_f), F32), pltpu.VMEM((2 * LANES, cap_c), F32)] * 2,
        compiler_params=pltpu.CompilerParams(collective_id=0, has_side_effects=True),
    )(*ints, *tables)
    return color.reshape(-1), trans.reshape(-1)


def solution(mesh):
    both = P(("morton", "level"))
    rows = P(("morton", "level"), None)
    coarse = P("morton", None)
    return jax.shard_map(
        shards,
        mesh=mesh,
        in_specs=(coarse, coarse, rows, rows, both, both, both, both, rows, both, both, both, both),
        out_specs=(both, both),
        check_vma=False,
    )
```

time: 52.1 us -> 42.8 us (0.82)
  Pallas kernels: 46.3 us -> 40.1 us
  other arithmetic: 3.58 us -> 0 us
  local copies, waits for them, and re-layouts: 1.11 us -> 1.86 us
    pallas_call x1, Pallas kernels: 46.3 us -> 40.1 us  [shards(): pl.pallas_call(functools.partial(frame_kernel, n_morton, n_level, cap_f,...]
    unnamed x12 -> x6, local copies, waits for them, and re-layouts: 0.03 us -> 1.86 us
    or x2 -> x0, other arithmetic: 1.44 us -> none  [pack(): return owner << CODE_BITS | code]
    mul x1 -> x0, other arithmetic: 1.35 us -> none  [shards(): trans = trans * parts[s, 1]]
    reshape x2 -> x0, local copies, waits for them, and re-layouts: 1.07 us -> none  [shards(): fine = fine.reshape(pixels, per_pixel).T]
    shift_left x1 -> x0, other arithmetic: 0.8 us -> none  [pack(): return owner << CODE_BITS | code]
where the time goes in v1:
time: 42.8 us; the launch traced here: 42.6 us
  Pallas kernels  40.1 us (94%)
  local copies, waits for them, and re-layouts  1.86 us (4%)
  between operations  0.65 us (2%)
    pallas_call x1, Pallas kernels, shards(): pl.pallas_call(functools.partial(frame_kernel, n_morton, n_level, cap_f,...  40.1 us
    unnamed x6, local copies, waits for them, and re-layouts  1.86 us

profile of v1, /device:TPU:0, one launch (start us, length us, event | category | flops | bytes accessed | tf_op | source)
XLA Modules:
  0.0 42.6 jit_solution(4904196578320477060)
XLA Ops:
  0.6 40.1 %shard_map.140 = (f32[2,128]{1,0:T(2,128)}, f32[2,128]{1,0:T(2,128)}) custom-call(s32[64,128]{1,0:T(8,128)} %bitcast.11, s32[64,128]{1,0:T(8,128)} %bitcast.12, s32[64,128]{1,0:T(8,128)} %bitcast.13, s32[64,128]{1,0:T(8,128)} %bitcast.14, s32[64,128]{1,0:T(8,128)} %bitcast.15, s32[8,128]{1,0:T(8,128)} %bitcast.16, s32[8,128]{1,0:T(8,128)} %bitcast.17, ...), custom_call_target="tpu_custom_call" | custom-call | tf_op jit(solution)/shard_map/pallas_call | solution.py:423
  40.7 0.0 copy-start.1
  40.7 0.7 %copy-done.1 = f32[2,128]{1,0:T(2,128)S(1)} copy-done((f32[2,128]{1,0:T(2,128)S(1)}, f32[2,128]{1,0:T(2,128)}, u32[]{:S(2)}) %copy-start.1) | copy-done | bytes 1048
  41.4 0.0 copy-start
  41.4 0.6 %copy.17 = f32[256]{0:T(256)} copy(f32[256]{0:T(256)S(1)} %bitcast.21) | data formatting | bytes 2048
  42.0 0.1 copy-done
  42.0 0.6 %copy.18 = f32[256]{0:T(256)} copy(f32[256]{0:T(256)S(1)} %bitcast.20) | data formatting | bytes 2048
Async XLA Ops:
  40.7 0.7 %copy-start.1 = (f32[2,128]{1,0:T(2,128)S(1)}, f32[2,128]{1,0:T(2,128)}, u32[]{:S(2)}) copy-start(f32[2,128]{1,0:T(2,128)} %get-tuple-element.4) | copy-start | bytes 3076
  41.4 0.6 %copy-start = (f32[2,128]{1,0:T(2,128)S(1)}, f32[2,128]{1,0:T(2,128)}, u32[]{:S(2)}) copy-start(f32[2,128]{1,0:T(2,128)} %get-tuple-element.5) | copy-start | bytes 3076

commit v2 on v1

--- a/solution.py
+++ b/solution.py
@@ -84,19 +84,48 @@
     return (rows & -BRICK) + 4 * (rows & 7) + ((rows >> 3) & 3)
 
 
-def turn_tables(pairs):
+def turned(turn, ref, parts):
+    return [dot_nt(turn, piece) for piece in split(ref[...], parts)]
+
+
+def turn_tables(ft_ref, fd_ref, fe_ref, ct_ref, cd_ref, ce_ref):
     turn = jnp.where(cells_of((LANES, LANES)) == iota((LANES, LANES), 1), 1.0, 0.0).astype(BF16)
-    for table_ref, dens_ref, emis_ref in pairs:
-        for at, ref in ((0, dens_ref), (LANES, emis_ref)):
-            for i, piece in enumerate(split(ref[...], 2)):
-                top = 2 * LANES * i + at
-                table_ref[top : top + LANES, :] = dot_nt(turn, piece).astype(BF16)
+    for at, ref in ((0, fd_ref), (LANES, fe_ref)):
+        for i, piece in enumerate(turned(turn, ref, 2)):
+            top = 2 * LANES * i + at
+            ft_ref[top : top + LANES, :] = piece.astype(BF16)
+    wide = ct_ref.shape[0] // PER_ROW
+    rows = cd_ref.shape[0]
+    for v, ref in enumerate((cd_ref, ce_ref)):
+        whole = sum(turned(turn, ref, 3))
+        for q in range(PER_ROW):
+            for at in range(0, rows, LANES):
+                size = min(LANES, rows - at)
+                top = q * wide + (at // LANES) * 2 * BRICK + v * BRICK
+                ct_ref[top : top + BRICK, :size] = whole[q * BRICK : (q + 1) * BRICK, at : at + size]
 
 
 def fetch(codes, table_ref, got_ref):
     ones = onehot(codes >> 13, table_ref.shape[1]).astype(BF16)
     both = dot_nn(table_ref[...], ones)
     got_ref[...] = both[: 2 * LANES] + both[2 * LANES :]
+
+
+def lanes_at(x, lanes):
+    return jnp.take_along_axis(x, lanes, axis=1)
+
+
+def front_to_back(dens, emis):
+    trans = [jnp.exp(-d) for d in dens]
+    color = [(1.0 - t) * e for t, e in zip(trans, emis)]
+    c, t = color[3], trans[3]
+    for k in (2, 1, 0):
+        c = color[k] + trans[k] * c
+        t = trans[k] * t
+    for shift in (1, 2, 4):
+        c = c + t * pltpu.roll(c, SUBS - shift, 0)
+        t = t * pltpu.roll(t, SUBS - shift, 0)
+    return c[0:1], t[0:1]
 
 
 def march(codes, got_ref, at):
@@ -108,17 +137,30 @@
     emis = jnp.where(inside, got_ref[LANES:, at : at + LANES], 0.0)
     dens = sum(dens[g * BRICK : (g + 1) * BRICK] for g in range(PER_ROW))
     emis = sum(emis[g * BRICK : (g + 1) * BRICK] for g in range(PER_ROW))
-    trans = jnp.exp(-dens)
-    color = (1.0 - trans) * emis
-    c, t = color[24:32], trans[24:32]
-    for k in (2, 1, 0):
-        tk = trans[8 * k : 8 * k + 8]
-        c = color[8 * k : 8 * k + 8] + tk * c
-        t = tk * t
-    for shift in (1, 2, 4):
-        c = c + t * pltpu.roll(c, 8 - shift, 0)
-        t = t * pltpu.roll(t, 8 - shift, 0)
-    return c[0:1], t[0:1]
+    steps = range(0, BRICK, SUBS)
+    return front_to_back([dens[k : k + SUBS] for k in steps], [emis[k : k + SUBS] for k in steps])
+
+
+def march_lanes(codes, table_ref):
+    codes = jnp.broadcast_to(codes, (SUBS, LANES))
+    row = codes >> 13
+    wide = table_ref.shape[0] // (PER_ROW * 2 * BRICK)
+    group = ((codes >> 11) & (PER_ROW - 1)) * wide + row // LANES
+    lane = row & (LANES - 1)
+    got = [None] * (2 * BRICK // SUBS)
+    for g in range(PER_ROW * wide):
+        here = group == g
+        for v in range(len(got)):
+            top = g * 2 * BRICK + v * SUBS
+            value = lanes_at(table_ref[top : top + SUBS, :], lane)
+            got[v] = value if g == 0 else jnp.where(here, value, got[v])
+    first = (codes >> 6) & (BRICK - 1)
+    last = first + (codes & 63)
+    steps = BRICK // SUBS
+    cells = [steps * iota((SUBS, LANES), 0) + k for k in range(steps)]
+    inside = [(c >= first) & (c < last) for c in cells]
+    dens = [jnp.where(m, x, 0.0) for m, x in zip(inside, got[:steps])]
+    return front_to_back(dens, got[steps:])
 
 
 def look_up(resp_ref, at, blocks, width, cell_ref, lane_ref, left_ref, out_refs):
@@ -143,10 +185,6 @@
             value = jnp.sum(jnp.where(here, total, 0.0), axis=0, keepdims=True)
             for j in range(chunk):
                 out_refs[v][r + j : r + j + 1, :] = value[:, j * LANES : (j + 1) * LANES]
-
-
-def lanes_at(x, lanes):
-    return jnp.take_along_axis(x, lanes, axis=1)
 
 
 def blend(per_pixel, fine_c, fine_t, coarse_c, coarse_t, slab_ref):
@@ -210,7 +248,7 @@
         in_sems,
         *refs,
     ) = refs
-    even, odd = refs[:2], refs[2:]
+    even, odd = refs
     n_dev = n_morton * n_level
     nf, nc = cap_f // LANES, cap_c // LANES
     blocks = nf + nc
@@ -232,6 +270,19 @@
 
     def before(k):
         return lax.rem(me + n_dev - k, n_dev)
+
+    early = max(n_dev // 4, 1)
+    late = n_dev - early
+    is_early = me < early
+    place_in = jnp.where(is_early, me, me - early)
+
+    def source(t):
+        one = lax.rem(me + t, early)
+        other = early + lax.rem(place_in + late + early - t, late)
+        return jnp.where(t == 0, me, jnp.where(t < early + jnp.where(is_early, 0, 1), one, other))
+
+    def steps_back(t):
+        return lax.rem(me + n_dev - source(t), n_dev)
 
     def ask(k):
         to = after(k)
@@ -311,39 +362,40 @@
     for copy in copies[9:]:
         copy.wait()
     fd_ref, fe_ref, cd_ref, ce_ref = table_refs
-    turn_tables(((ft_ref, fd_ref, fe_ref), (ct_ref, cd_ref, ce_ref)))
+    turn_tables(ft_ref, fd_ref, fe_ref, ct_ref, cd_ref, ce_ref)
 
     def codes_of(i, at, rows):
         return jnp.concatenate([code_ref[i, at + r : at + r + 1, :] for r in range(rows)], axis=1)
 
-    def fetch_source(i, bufs):
-        fetch(codes_of(i, 0, nf), ft_ref, bufs[0])
-        fetch(codes_of(i, nf, nc), ct_ref, bufs[1])
-
-    def march_source(i, bufs):
-        for b in range(blocks):
-            buf, at = (bufs[0], b) if b < nf else (bufs[1], b - nf)
-            c, t = march(code_ref[i, b : b + 1, :], buf, at * LANES)
-            served_ref[i, b : b + 1, :] = c
-            served_ref[i, blocks + b : blocks + b + 1, :] = t
-
-    for ref in odd:
-        ref[...] = jnp.zeros(ref.shape, F32)
+    def put(i, b, c, t):
+        served_ref[i, b : b + 1, :] = c
+        served_ref[i, blocks + b : blocks + b + 1, :] = t
+
+    def fetch_source(i, buf):
+        fetch(codes_of(i, 0, nf), ft_ref, buf)
+        for b in range(nf, blocks):
+            put(i, b, *march_lanes(code_ref[i, b : b + 1, :], ct_ref))
+
+    def march_source(i, buf):
+        for b in range(nf):
+            put(i, b, *march(code_ref[i, b : b + 1, :], buf, b * LANES))
+
+    odd[...] = jnp.zeros(odd.shape, F32)
 
     def two_sources(j, _):
         for u in range(2):
 
             @pl.when(2 * j + u > 0)
             def _():
-                ask(2 * j + u).wait_recv()
+                ask(steps_back(2 * j + u)).wait_recv()
 
             @pl.when(2 * j - 3 + u > 0)
             def _():
-                tell(2 * j - 3 + u).start()
-
-        now, later = before(2 * j), before(2 * j + 1)
+                tell(steps_back(2 * j - 3 + u)).start()
+
+        now, later = source(2 * j), source(2 * j + 1)
         fetch_source(now, even)
-        march_source(before(jnp.maximum(2 * j - 1, 0)), odd)
+        march_source(source(jnp.maximum(2 * j - 1, 0)), odd)
         fetch_source(later, odd)
         march_source(now, even)
         return 0
@@ -351,9 +403,9 @@
     lax.fori_loop(0, n_dev // 2, two_sources, 0)
     for k in (n_dev - 3, n_dev - 2):
         if k > 0:
-            tell(k).start()
-    march_source(before(n_dev - 1), odd)
-    tell(n_dev - 1).start()
+            tell(steps_back(k)).start()
+    march_source(source(n_dev - 1), odd)
+    tell(steps_back(n_dev - 1)).start()
     resp_ref[me] = served_ref[me]
     rank = frank_ref[...]
     wf, wc = min(nf, 2), min(nc, 2)
@@ -432,7 +484,7 @@
             pltpu.VMEM((wide, LANES), BF16),
             pltpu.VMEM((wide, 2 * LANES), F32),
             pltpu.VMEM((4 * LANES, t_rows), BF16),
-            pltpu.VMEM((4 * LANES, g_rows), BF16),
+            pltpu.VMEM((-(-g_rows // LANES) * PER_ROW * 2 * BRICK, LANES), F32),
             pltpu.VMEM((left_rows, 2 * LANES), BF16),
         ]
         + [pltpu.VMEM((f_rows, LANES), F32)] * 2
@@ -447,7 +499,7 @@
         ]
         + sems
         + [pltpu.SemaphoreType.DMA((13,))]
-        + [pltpu.VMEM((2 * LANES, cap_f), F32), pltpu.VMEM((2 * LANES, cap_c), F32)] * 2,
+        + [pltpu.VMEM((2 * LANES, cap_f), F32)] * 2,
         compiler_params=pltpu.CompilerParams(collective_id=0, has_side_effects=True),
     )(*ints, *tables)
     return color.reshape(-1), trans.reshape(-1)

time: 42.8 us -> 38.6 us (0.902)
  the two profiles are of different devices: /device:TPU:0 before, /device:TPU:13 now
where the time goes in v2:
time: 38.6 us; the launch traced here: 38.4 us
  Pallas kernels  35.8 us (93%)
  local copies, waits for them, and re-layouts  1.86 us (5%)
  between operations  0.65 us (2%)
    pallas_call x1, Pallas kernels, shards(): pl.pallas_call(functools.partial(frame_kernel, n_morton, n_level, cap_f,...  35.8 us
    unnamed x6, local copies, waits for them, and re-layouts  1.86 us

profile of v2, /device:TPU:13, one launch (start us, length us, event | category | flops | bytes accessed | tf_op | source)
XLA Modules:
  0.0 38.4 jit_solution(8022469698426926432)
XLA Ops:
  0.6 35.8 %shard_map.140 = (f32[2,128]{1,0:T(2,128)}, f32[2,128]{1,0:T(2,128)}) custom-call(s32[64,128]{1,0:T(8,128)} %bitcast.11, s32[64,128]{1,0:T(8,128)} %bitcast.12, s32[64,128]{1,0:T(8,128)} %bitcast.13, s32[64,128]{1,0:T(8,128)} %bitcast.14, s32[64,128]{1,0:T(8,128)} %bitcast.15, s32[8,128]{1,0:T(8,128)} %bitcast.16, s32[8,128]{1,0:T(8,128)} %bitcast.17, ...), custom_call_target="tpu_custom_call" | custom-call | tf_op jit(solution)/shard_map/pallas_call | solution.py:475
  36.5 0.0 copy-start.1
  36.5 0.7 %copy-done.1 = f32[2,128]{1,0:T(2,128)S(1)} copy-done((f32[2,128]{1,0:T(2,128)S(1)}, f32[2,128]{1,0:T(2,128)}, u32[]{:S(2)}) %copy-start.1) | copy-done | bytes 1048
  37.2 0.0 copy-start
  37.2 0.6 %copy.17 = f32[256]{0:T(256)} copy(f32[256]{0:T(256)S(1)} %bitcast.21) | data formatting | bytes 2048
  37.7 0.1 copy-done
  37.8 0.6 %copy.18 = f32[256]{0:T(256)} copy(f32[256]{0:T(256)S(1)} %bitcast.20) | data formatting | bytes 2048
Async XLA Ops:
  36.5 0.7 %copy-start.1 = (f32[2,128]{1,0:T(2,128)S(1)}, f32[2,128]{1,0:T(2,128)}, u32[]{:S(2)}) copy-start(f32[2,128]{1,0:T(2,128)} %get-tuple-element.4) | copy-start | bytes 3076
  37.2 0.6 %copy-start = (f32[2,128]{1,0:T(2,128)S(1)}, f32[2,128]{1,0:T(2,128)}, u32[]{:S(2)}) copy-start(f32[2,128]{1,0:T(2,128)} %get-tuple-element.5) | copy-start | bytes 3076

commit v3 on v2

--- a/solution.py
+++ b/solution.py
@@ -65,18 +65,31 @@
         carry = carry + part[:, LANES:]
 
 
+def to_float(value):
+    return ((LANES + (value & (LANES - 1))) << (value >> 7)).astype(F32)
+
+
+def from_float(x):
+    y = x.astype(I32)
+    shift = jnp.zeros_like(y)
+    for bits in (8, 4, 2, 1):
+        over = y >= (LANES << bits)
+        y = jnp.where(over, y >> bits, y)
+        shift = jnp.where(over, shift + bits, shift)
+    return jnp.where(y == 0, 0, y - LANES + (shift << 7))
+
+
 def place(cell_ref, lane_ref, code_ref, cells, chunk):
     rows = cell_ref.shape[0]
-    placed = jnp.zeros((3 * cells, LANES), F32)
+    placed = jnp.zeros((2 * cells, LANES), F32)
     for r in range(0, rows, chunk):
         here = iota((cells, chunk * LANES), 0) == across(cell_ref, r, chunk)
         code = across(code_ref, r, chunk)
-        pieces = [code & 255, (code >> 8) & 255, code >> 16]
-        left = jnp.concatenate([jnp.where(here, p.astype(F32), 0.0).astype(BF16) for p in pieces], axis=0)
+        pieces = [to_float(code >> 11), to_float(code & 2047)]
+        left = jnp.concatenate([jnp.where(here, p, 0.0).astype(BF16) for p in pieces], axis=0)
         right = onehot(across(lane_ref, r, chunk), LANES).astype(BF16)
         placed = placed + dot_nt(left, right)
-    a, b, c = (placed[i * cells : (i + 1) * cells].astype(I32) for i in range(3))
-    return a + (b << 8) + (c << 16)
+    return (from_float(placed[:cells]) << 11) + from_float(placed[cells:])
 
 
 def cells_of(shape):
@@ -211,7 +224,7 @@
 
 
 def frame_kernel(n_morton, n_level, cap_f, cap_c, *refs):
-    ints, tables, (color_ref, trans_ref), refs = refs[:9], refs[9:13], refs[13:15], refs[15:]
+    ints, tables, out_ref, refs = refs[:9], refs[9:13], refs[13], refs[14:]
     int_refs, table_refs, refs = refs[:9], refs[9:13], refs[13:]
     (
         owner_ref,
@@ -265,46 +278,61 @@
     def device(d):
         return d // n_level, lax.rem(d, n_level)
 
-    def after(k):
-        return lax.rem(me + k, n_dev)
-
-    def before(k):
-        return lax.rem(me + n_dev - k, n_dev)
-
-    early = max(n_dev // 4, 1)
-    late = n_dev - early
-    is_early = me < early
-    place_in = jnp.where(is_early, me, me - early)
-
-    def source(t):
-        one = lax.rem(me + t, early)
-        other = early + lax.rem(place_in + late + early - t, late)
-        return jnp.where(t == 0, me, jnp.where(t < early + jnp.where(is_early, 0, 1), one, other))
-
-    def steps_back(t):
-        return lax.rem(me + n_dev - source(t), n_dev)
-
-    def ask(k):
-        to = after(k)
+    def wrap(x, n):
+        return jnp.where(x >= n, x - n, x)
+
+    def others(act):
+        levels = [wrap(level + k, n_level) for k in range(n_level)]
+        for there in levels[1:]:
+            act(morton, there)
+
+        def group(k, _):
+            for there in levels:
+                act(wrap(morton + k, n_morton), there)
+            return 0
+
+        lax.fori_loop(1, n_morton, group, 0)
+
+    def ask(there, source):
         return pltpu.make_async_remote_copy(
-            src_ref=msg_ref.at[to],
+            src_ref=msg_ref.at[there[0] * n_level + there[1]],
             dst_ref=code_ref.at[me],
-            send_sem=ask_send.at[k],
-            recv_sem=ask_recv.at[k],
-            device_id=device(to),
+            send_sem=ask_send.at[there[0] * n_level + there[1]],
+            recv_sem=ask_recv.at[source],
+            device_id=there,
             device_id_type=mesh_ids,
         )
 
-    def tell(k):
-        to = before(k)
+    def tell(there, source):
         return pltpu.make_async_remote_copy(
-            src_ref=served_ref.at[to],
+            src_ref=served_ref.at[there[0] * n_level + there[1]],
             dst_ref=resp_ref.at[me],
-            send_sem=tell_send.at[k],
-            recv_sem=tell_recv.at[k],
-            device_id=device(to),
+            send_sem=tell_send.at[there[0] * n_level + there[1]],
+            recv_sem=tell_recv.at[source],
+            device_id=there,
             device_id_type=mesh_ids,
         )
+
+    partner = level + 1 - 2 * lax.rem(level, 2)
+    row, column_in = morton // 2, lax.rem(morton, 2)
+    ordered = n_morton % 2 == 0 and n_morton >= 6 and n_level % 2 == 0
+
+    def source(t):
+        if not ordered:
+            return lax.rem(me + n_dev - t, n_dev)
+        n_rows = n_morton // 2
+        g, turn = (t - 1) // n_level, lax.rem(t - 1, n_level)
+        first = row == 0
+        u = jnp.maximum(jnp.where(first, g - 1, g - 2), 0)
+        far = 2 * (1 + lax.rem(row + u // 2, n_rows - 1)) + lax.rem(u + column_in, 2)
+        head = jnp.where(first, g < 1, g < 2)
+        group = jnp.where(head, jnp.where(first, 1 - column_in, g), far)
+        group = jnp.where((row > 0) & (g == n_morton - 2), 2 * row + 1 - column_in, group)
+        i = t - (n_dev - n_level + 1)
+        near = jnp.where(lax.rem(i, 2) == 0, level, partner) + 2 * (i // 2 + 1)
+        near = jnp.where(t == n_dev - 1, partner, lax.rem(near, n_level))
+        away = group * n_level + wrap(level + turn, n_level)
+        return jnp.where(t == 0, me, jnp.where(i >= 0, morton * n_level + near, away))
 
     def join(k):
         to = lax.rem(level + k, n_level)
@@ -317,6 +345,9 @@
             device_id_type=mesh_ids,
         )
 
+    def after(k):
+        return wrap(me + k, n_dev)
+
     barrier = pltpu.get_barrier_semaphore()
 
     def each(low, high, act):
@@ -326,7 +357,7 @@
 
         lax.fori_loop(low, high, body, 0)
 
-    each(1, n_dev, lambda k: pl.semaphore_signal(barrier, inc=1, device_id=device(after(k)), device_id_type=mesh_ids))
+    others(lambda m, l: pl.semaphore_signal(barrier, inc=1, device_id=(m, l), device_id_type=mesh_ids))
     for copy in copies[9:]:
         copy.start()
     for copy in copies[:9]:
@@ -357,7 +388,7 @@
         msg_ref[i, nf:, :] = coarse_msg[i * nc : (i + 1) * nc]
 
     pl.semaphore_wait(barrier, n_dev - 1)
-    each(1, n_dev, lambda k: ask(k).start())
+    others(lambda m, l: ask((m, l), me).start())
     code_ref[me] = msg_ref[me]
     for copy in copies[9:]:
         copy.wait()
@@ -382,30 +413,42 @@
 
     odd[...] = jnp.zeros(odd.shape, F32)
 
-    def two_sources(j, _):
-        for u in range(2):
-
-            @pl.when(2 * j + u > 0)
-            def _():
-                ask(steps_back(2 * j + u)).wait_recv()
-
-            @pl.when(2 * j - 3 + u > 0)
-            def _():
-                tell(steps_back(2 * j - 3 + u)).start()
-
-        now, later = source(2 * j), source(2 * j + 1)
+    def await_ask(d):
+        ask((morton, level), d).wait_recv()
+
+    def start_tell(d):
+        tell(device(d), me).start()
+
+    def two_sources(j, state):
+        older, old, last, now, later = state
+
+        @pl.when(j > 0)
+        def _():
+            await_ask(now)
+
+        @pl.when(j > 1)
+        def _():
+            start_tell(older)
+
+        await_ask(later)
+
+        @pl.when(j > 1)
+        def _():
+            start_tell(old)
+
         fetch_source(now, even)
-        march_source(source(jnp.maximum(2 * j - 1, 0)), odd)
+        march_source(last, odd)
         fetch_source(later, odd)
         march_source(now, even)
-        return 0
-
-    lax.fori_loop(0, n_dev // 2, two_sources, 0)
-    for k in (n_dev - 3, n_dev - 2):
-        if k > 0:
-            tell(steps_back(k)).start()
-    march_source(source(n_dev - 1), odd)
-    tell(steps_back(n_dev - 1)).start()
+        ahead = jnp.minimum(2 * j + 2, n_dev - 2)
+        return last, now, later, source(ahead), source(ahead + 1)
+
+    state = (me, me, me, me, source(1))
+    older, old, last, _, _ = lax.fori_loop(0, n_dev // 2, two_sources, state)
+    start_tell(older)
+    start_tell(old)
+    march_source(last, odd)
+    start_tell(last)
     resp_ref[me] = served_ref[me]
     rank = frank_ref[...]
     wf, wc = min(nf, 2), min(nc, 2)
@@ -415,24 +458,24 @@
     slot = rank // n_level
     ccell_ref[...] = group_ref[...] * n_level + (rank & (n_level - 1)) + (slot // (wc * LANES)) * n_dev
     clane_ref[...] = slot & (wc * LANES - 1)
-    each(1, n_dev, lambda k: tell(k).wait_recv())
+    each(1, n_dev, lambda k: tell((morton, level), after(k)).wait_recv())
     look_up(resp_ref, nf, nc, wc, ccell_ref, clane_ref, left_ref, (cc_ref, ctr_ref))
     look_up(resp_ref, 0, nf, wf, fcell_ref, flane_ref, left_ref, (fc_ref, ftr_ref))
     blend(owner_ref.shape[0] // group_ref.shape[0], fc_ref, ftr_ref, cc_ref, ctr_ref, slab_ref)
     for k in range(1, n_level):
         join(k).start()
     slabs_ref[level] = slab_ref[level]
-    each(1, n_dev, lambda k: ask(k).wait_send())
-    each(1, n_dev, lambda k: tell(k).wait_send())
+    each(1, n_dev, lambda k: ask(device(after(k)), me).wait_send())
+    each(1, n_dev, lambda k: tell(device(after(k)), me).wait_send())
     for k in range(1, n_level):
         join(k).wait()
-    rows = color_ref.shape[0]
+    rows = out_ref.shape[1]
     color, trans = slabs_ref[0, :rows, :], slabs_ref[0, rows:, :]
     for s in range(1, n_level):
         color = color + trans * slabs_ref[s, :rows, :]
         trans = trans * slabs_ref[s, rows:, :]
-    color_ref[...] = color
-    trans_ref[...] = trans
+    out_ref[0] = color
+    out_ref[1] = trans
 
 
 def shards(
@@ -472,11 +515,11 @@
         return pltpu.VMEM(x.shape, x.dtype)
 
     sems = [pltpu.SemaphoreType.DMA((n_dev,))] * 4 + [pltpu.SemaphoreType.DMA((n_level,))] * 2
-    color, trans = pl.pallas_call(
+    image = pl.pallas_call(
         functools.partial(frame_kernel, n_morton, n_level, cap_f, cap_c),
-        out_shape=[jax.ShapeDtypeStruct((level_rows, LANES), F32)] * 2,
+        out_shape=jax.ShapeDtypeStruct((2, level_rows, LANES), F32),
         in_specs=[ANY] * 13,
-        out_specs=[VMEM] * 2,
+        out_specs=VMEM,
         scratch_shapes=[like(x) for x in ints + tables]
         + [pltpu.VMEM((f_rows, LANES), I32)] * 5
         + [pltpu.VMEM((c_rows, LANES), I32)] * 5
@@ -502,7 +545,7 @@
         + [pltpu.VMEM((2 * LANES, cap_f), F32)] * 2,
         compiler_params=pltpu.CompilerParams(collective_id=0, has_side_effects=True),
     )(*ints, *tables)
-    return color.reshape(-1), trans.reshape(-1)
+    return image[0].reshape(-1), image[1].reshape(-1)
 
 
 def solution(mesh):

time: 38.6 us -> 35.9 us (0.930)
  the two profiles are of different devices: /device:TPU:13 before, /device:TPU:0 now
where the time goes in v3:
time: 35.9 us; the launch traced here: 35.7 us
  Pallas kernels  33.8 us (94%)
  local copies, waits for them, and re-layouts  1.24 us (3%)
  between operations  0.64 us (2%)
    pallas_call x1, Pallas kernels, shards(): pl.pallas_call(functools.partial(frame_kernel, n_morton, n_level, cap_f,...  33.8 us
    another operation x1, local copies, waits for them, and re-layouts, shards(): return (image[0].reshape(-1), image[1].reshape(-1))  1.24 us

profile of v3, /device:TPU:0, one launch (start us, length us, event | category | flops | bytes accessed | tf_op | source)
XLA Modules:
  0.0 35.7 jit_solution(16131633590190231851)
XLA Ops:
  0.6 33.8 %shard_map.140 = f32[2,2,128]{2,1,0:T(2,128)} custom-call(s32[64,128]{1,0:T(8,128)} %bitcast.13, s32[64,128]{1,0:T(8,128)} %bitcast.14, s32[64,128]{1,0:T(8,128)} %bitcast.15, s32[64,128]{1,0:T(8,128)} %bitcast.16, s32[64,128]{1,0:T(8,128)} %bitcast.17, s32[8,128]{1,0:T(8,128)} %bitcast.18, s32[8,128]{1,0:T(8,128)} %bitcast.19, s32[8,128]{1,0:T(8,128)} %bitcast.20, ...), custom_call_target="tpu_custom_call" | custom-call | tf_op jit(solution)/shard_map/pallas_call | solution.py:518
  34.5 1.2 %slice_bitcast_fusion = (f32[256]{0:T(256)}, f32[256]{0:T(256)}) fusion(f32[2,2,128]{2,1,0:T(2,128)} %shard_map.140), kind=kLoop, calls=%fused_computation | loop fusion | bytes 4096 | tf_op jit(solution)/shard_map/reshape;squeeze | solution.py:548

commit v4 on v3

--- a/solution.py
+++ b/solution.py
@@ -15,6 +15,7 @@
 F32 = jnp.float32
 BF16 = jnp.bfloat16
 I32 = jnp.int32
+I16 = jnp.int16
 VMEM = pl.BlockSpec(memory_space=pltpu.VMEM)
 ANY = pl.BlockSpec(memory_space=pl.ANY)
 
@@ -23,8 +24,12 @@
     return lax.broadcasted_iota(I32, shape, dim)
 
 
+def equals(ids, width):
+    return iota((width, ids.shape[1]), 0).astype(I16) == ids.astype(I16)
+
+
 def onehot(ids, width):
-    return jnp.where(iota((width, ids.shape[1]), 0) == ids, 1.0, 0.0).astype(F32)
+    return jnp.where(equals(ids, width), jnp.ones((), BF16), jnp.zeros((), BF16))
 
 
 def split(x, parts):
@@ -51,7 +56,7 @@
 def rank_rows(ids_ref, width, ones_ref, within_ref, out_ref):
     rows = ids_ref.shape[0]
     for r in range(rows):
-        ones_ref[r * width : (r + 1) * width, :] = onehot(ids_ref[r : r + 1, :], width).astype(BF16)
+        ones_ref[r * width : (r + 1) * width, :] = onehot(ids_ref[r : r + 1, :], width)
     lane, other = iota((LANES, 2 * LANES), 0), iota((LANES, 2 * LANES), 1)
     counter = jnp.where((lane < other) | (other >= LANES), 1.0, 0.0).astype(BF16)
     used = rows * width
@@ -83,11 +88,11 @@
     rows = cell_ref.shape[0]
     placed = jnp.zeros((2 * cells, LANES), F32)
     for r in range(0, rows, chunk):
-        here = iota((cells, chunk * LANES), 0) == across(cell_ref, r, chunk)
+        here = equals(across(cell_ref, r, chunk), cells)
         code = across(code_ref, r, chunk)
-        pieces = [to_float(code >> 11), to_float(code & 2047)]
-        left = jnp.concatenate([jnp.where(here, p, 0.0).astype(BF16) for p in pieces], axis=0)
-        right = onehot(across(lane_ref, r, chunk), LANES).astype(BF16)
+        pieces = [to_float(code >> 11).astype(BF16), to_float(code & 2047).astype(BF16)]
+        left = jnp.concatenate([jnp.where(here, p, jnp.zeros((), BF16)) for p in pieces], axis=0)
+        right = onehot(across(lane_ref, r, chunk), LANES)
         placed = placed + dot_nt(left, right)
     return (from_float(placed[:cells]) << 11) + from_float(placed[cells:])
 
@@ -119,7 +124,7 @@
 
 
 def fetch(codes, table_ref, got_ref):
-    ones = onehot(codes >> 13, table_ref.shape[1]).astype(BF16)
+    ones = onehot(codes >> 13, table_ref.shape[1])
     both = dot_nn(table_ref[...], ones)
     got_ref[...] = both[: 2 * LANES] + both[2 * LANES :]
 
@@ -176,28 +181,49 @@
     return front_to_back(dens, got[steps:])
 
 
-def look_up(resp_ref, at, blocks, width, cell_ref, lane_ref, left_ref, out_refs):
-    n_dev, half = resp_ref.shape[0], resp_ref.shape[1] // 2
+def look_up(resp_ref, near, at, blocks, width, owner_ref, rank_ref, left_ref, out_refs):
+    half = resp_ref.shape[1] // 2
+    owners = resp_ref.shape[0] - near
     high = blocks // width
-    cells = high * n_dev
+    cells = high * owners
     for v in range(2):
         for h in range(high):
             for w in range(width):
-                full = resp_ref[:, v * half + at + h * width + w, :]
+                full = resp_ref[near:, v * half + at + h * width + w, :]
                 for i, piece in enumerate(split(full, 2)):
-                    top = (2 * v + i) * cells + h * n_dev
-                    left_ref[top : top + n_dev, w * LANES : (w + 1) * LANES] = piece
-    rows = cell_ref.shape[0]
+                    top = (2 * v + i) * cells + h * owners
+                    left_ref[top : top + owners, w * LANES : (w + 1) * LANES] = piece
+    rows = owner_ref.shape[0]
     chunk = SUBS
     left = left_ref[: 4 * cells, : width * LANES]
     for r in range(0, rows, chunk):
-        got = dot_nn(left, onehot(across(lane_ref, r, chunk), width * LANES).astype(BF16))
-        here = iota((cells, chunk * LANES), 0) == across(cell_ref, r, chunk)
+        owner, rank = across(owner_ref, r, chunk), across(rank_ref, r, chunk)
+        got = dot_nn(left, onehot(rank & (width * LANES - 1), width * LANES))
+        cell = jnp.where(owner >= near, owner - near + rank // (width * LANES) * owners, -1)
+        here = iota((cells, chunk * LANES), 0) == cell
         for v in range(2):
             total = got[2 * v * cells : (2 * v + 1) * cells] + got[(2 * v + 1) * cells : (2 * v + 2) * cells]
             value = jnp.sum(jnp.where(here, total, 0.0), axis=0, keepdims=True)
             for j in range(chunk):
                 out_refs[v][r + j : r + j + 1, :] = value[:, j * LANES : (j + 1) * LANES]
+
+
+def look_near(resp_ref, near, at, blocks, owner_ref, rank_ref, out_refs):
+    half = resp_ref.shape[1] // 2
+    for r in range(0, owner_ref.shape[0], SUBS):
+        rank = rank_ref[r : r + SUBS, :]
+        cell = owner_ref[r : r + SUBS, :] * blocks + rank // LANES
+        lane = rank & (LANES - 1)
+        values = [ref[r : r + SUBS, :] for ref in out_refs]
+        for d in range(near):
+            for b in range(blocks):
+                here = cell == d * blocks + b
+                for v in range(2):
+                    row = resp_ref[d, v * half + at + b : v * half + at + b + 1, :]
+                    value = lanes_at(jnp.broadcast_to(row, (SUBS, LANES)), lane)
+                    values[v] = jnp.where(here, value, values[v])
+        for ref, value in zip(out_refs, values):
+            ref[r : r + SUBS, :] = value
 
 
 def blend(per_pixel, fine_c, fine_t, coarse_c, coarse_t, slab_ref):
@@ -306,33 +332,38 @@
     def tell(there, source):
         return pltpu.make_async_remote_copy(
             src_ref=served_ref.at[there[0] * n_level + there[1]],
-            dst_ref=resp_ref.at[me],
+            dst_ref=resp_ref.at[source],
             send_sem=tell_send.at[there[0] * n_level + there[1]],
             recv_sem=tell_recv.at[source],
             device_id=there,
             device_id_type=mesh_ids,
         )
 
+    ordered = n_morton % 2 == 0 and n_morton >= 6 and n_level % 2 == 0
+    near = 2 * n_level if ordered else 0
     partner = level + 1 - 2 * lax.rem(level, 2)
     row, column_in = morton // 2, lax.rem(morton, 2)
-    ordered = n_morton % 2 == 0 and n_morton >= 6 and n_level % 2 == 0
+
+    def seen_by(d, m):
+        return wrap(d + n_dev - m // 2 * near, n_dev)
 
     def source(t):
         if not ordered:
             return lax.rem(me + n_dev - t, n_dev)
         n_rows = n_morton // 2
-        g, turn = (t - 1) // n_level, lax.rem(t - 1, n_level)
+        step = jnp.maximum(t - 2, 0)
+        g, turn = step // n_level, lax.rem(step, n_level)
         first = row == 0
         u = jnp.maximum(jnp.where(first, g - 1, g - 2), 0)
         far = 2 * (1 + lax.rem(row + u // 2, n_rows - 1)) + lax.rem(u + column_in, 2)
         head = jnp.where(first, g < 1, g < 2)
         group = jnp.where(head, jnp.where(first, 1 - column_in, g), far)
         group = jnp.where((row > 0) & (g == n_morton - 2), 2 * row + 1 - column_in, group)
-        i = t - (n_dev - n_level + 1)
-        near = jnp.where(lax.rem(i, 2) == 0, level, partner) + 2 * (i // 2 + 1)
-        near = jnp.where(t == n_dev - 1, partner, lax.rem(near, n_level))
+        i = t - (n_dev - n_level + 2)
+        beside = lax.rem(jnp.where(lax.rem(i, 2) == 0, level, partner) + 2 * (i // 2 + 1), n_level)
         away = group * n_level + wrap(level + turn, n_level)
-        return jnp.where(t == 0, me, jnp.where(i >= 0, morton * n_level + near, away))
+        far_or_beside = jnp.where(i >= 0, morton * n_level + beside, away)
+        return jnp.where(t == 0, me, jnp.where(t == 1, morton * n_level + partner, far_or_beside))
 
     def join(k):
         to = lax.rem(level + k, n_level)
@@ -417,7 +448,8 @@
         ask((morton, level), d).wait_recv()
 
     def start_tell(d):
-        tell(device(d), me).start()
+        there = device(d)
+        tell(there, seen_by(me, there[0])).start()
 
     def two_sources(j, state):
         older, old, last, now, later = state
@@ -449,18 +481,32 @@
     start_tell(old)
     march_source(last, odd)
     start_tell(last)
-    resp_ref[me] = served_ref[me]
-    rank = frank_ref[...]
-    wf, wc = min(nf, 2), min(nc, 2)
-    fcell_ref[...] = owner_ref[...] + (rank // (wf * LANES)) * n_dev
-    flane_ref[...] = rank & (wf * LANES - 1)
+    mine = seen_by(me, morton)
+    resp_ref[mine] = served_ref[me]
+    seen = owner_ref[...] - row * near
+    owner_ref[...] = jnp.where(seen < 0, seen + n_dev, seen)
     rank = crank_ref[...]
-    slot = rank // n_level
-    ccell_ref[...] = group_ref[...] * n_level + (rank & (n_level - 1)) + (slot // (wc * LANES)) * n_dev
-    clane_ref[...] = slot & (wc * LANES - 1)
-    each(1, n_dev, lambda k: tell((morton, level), after(k)).wait_recv())
-    look_up(resp_ref, nf, nc, wc, ccell_ref, clane_ref, left_ref, (cc_ref, ctr_ref))
-    look_up(resp_ref, 0, nf, wf, fcell_ref, flane_ref, left_ref, (fc_ref, ftr_ref))
+    seen = group_ref[...] * n_level + (rank & (n_level - 1)) - row * near
+    ccell_ref[...] = jnp.where(seen < 0, seen + n_dev, seen)
+    crank_ref[...] = rank // n_level
+
+    def await_tells(low, high):
+        def one(v, _):
+            @pl.when(v != mine)
+            def _():
+                tell((morton, level), v).wait_recv()
+
+            return 0
+
+        lax.fori_loop(low, high, one, 0)
+
+    await_tells(near, n_dev)
+    fine, coarse = (owner_ref, frank_ref), (ccell_ref, crank_ref)
+    look_up(resp_ref, near, nf, nc, min(nc, 2), *coarse, left_ref, (cc_ref, ctr_ref))
+    look_up(resp_ref, near, 0, nf, min(nf, 2), *fine, left_ref, (fc_ref, ftr_ref))
+    await_tells(0, near)
+    look_near(resp_ref, near, nf, nc, *coarse, (cc_ref, ctr_ref))
+    look_near(resp_ref, near, 0, nf, *fine, (fc_ref, ftr_ref))
     blend(owner_ref.shape[0] // group_ref.shape[0], fc_ref, ftr_ref, cc_ref, ctr_ref, slab_ref)
     for k in range(1, n_level):
         join(k).start()

time: 35.9 us -> 32.3 us (0.90); the launches traced: 35.7 us -> 31.7 us
  Pallas kernels: 33.8 us -> 29.8 us
    pallas_call x1, Pallas kernels: 33.8 us -> 29.8 us  [shards(): pl.pallas_call(functools.partial(frame_kernel, n_morton, n_level, cap_f,...]
where the time goes in v4:
time: 32.3 us; the launch traced here: 31.7 us
  Pallas kernels  29.8 us (92%)
  local copies, waits for them, and re-layouts  1.24 us (4%)
  between operations  0.64 us (2%)
    pallas_call x1, Pallas kernels, shards(): pl.pallas_call(functools.partial(frame_kernel, n_morton, n_level, cap_f,...  29.8 us
    another operation x1, local copies, waits for them, and re-layouts, shards(): return (image[0].reshape(-1), image[1].reshape(-1))  1.24 us

profile of v4, /device:TPU:0, one launch (start us, length us, event | category | flops | bytes accessed | tf_op | source)
XLA Modules:
  0.0 31.7 jit_solution(10906028402699551271)
XLA Ops:
  0.6 29.8 %shard_map.140 = f32[2,2,128]{2,1,0:T(2,128)} custom-call(s32[64,128]{1,0:T(8,128)} %bitcast.13, s32[64,128]{1,0:T(8,128)} %bitcast.14, s32[64,128]{1,0:T(8,128)} %bitcast.15, s32[64,128]{1,0:T(8,128)} %bitcast.16, s32[64,128]{1,0:T(8,128)} %bitcast.17, s32[8,128]{1,0:T(8,128)} %bitcast.18, s32[8,128]{1,0:T(8,128)} %bitcast.19, s32[8,128]{1,0:T(8,128)} %bitcast.20, ...), custom_call_target="tpu_custom_call" | custom-call | tf_op jit(solution)/shard_map/pallas_call | solution.py:564
  30.4 1.2 %slice_bitcast_fusion = (f32[256]{0:T(256)}, f32[256]{0:T(256)}) fusion(f32[2,2,128]{2,1,0:T(2,128)} %shard_map.140), kind=kLoop, calls=%fused_computation | loop fusion | bytes 4096 | tf_op jit(solution)/shard_map/reshape;squeeze | solution.py:594

commit v5 on v4

--- a/solution.py
+++ b/solution.py
@@ -147,16 +147,30 @@
 
 
 def march(codes, got_ref, at):
-    first = (codes >> 6) & 127
+    codes = jnp.broadcast_to(codes, (SUBS, LANES))
+    quarter = (codes >> 11) & (PER_ROW - 1)
+    here = [quarter == q for q in range(PER_ROW - 1)]
+    steps = BRICK // SUBS
+
+    def column(top):
+        out = []
+        for k in range(steps):
+            rows = [got_ref[top + q * BRICK + k * SUBS : top + q * BRICK + (k + 1) * SUBS, at : at + LANES] for q in range(PER_ROW)]
+            x = rows[-1]
+            for q in range(PER_ROW - 1):
+                x = jnp.where(here[q], rows[q], x)
+            out.append(x)
+        return out
+
+    return front_to_back(sampled(codes, column(0)), column(LANES))
+
+
+def sampled(codes, dens):
+    first = (codes >> 6) & (BRICK - 1)
     last = first + (codes & 63)
-    cells = cells_of((LANES, LANES))
-    inside = (cells >= first) & (cells < last)
-    dens = jnp.where(inside, got_ref[:LANES, at : at + LANES], 0.0)
-    emis = jnp.where(inside, got_ref[LANES:, at : at + LANES], 0.0)
-    dens = sum(dens[g * BRICK : (g + 1) * BRICK] for g in range(PER_ROW))
-    emis = sum(emis[g * BRICK : (g + 1) * BRICK] for g in range(PER_ROW))
-    steps = range(0, BRICK, SUBS)
-    return front_to_back([dens[k : k + SUBS] for k in steps], [emis[k : k + SUBS] for k in steps])
+    steps = BRICK // SUBS
+    cells = [steps * iota((SUBS, LANES), 0) + k for k in range(steps)]
+    return [jnp.where((c >= first) & (c < last), x, 0.0) for c, x in zip(cells, dens)]
 
 
 def march_lanes(codes, table_ref):
@@ -172,13 +186,8 @@
             top = g * 2 * BRICK + v * SUBS
             value = lanes_at(table_ref[top : top + SUBS, :], lane)
             got[v] = value if g == 0 else jnp.where(here, value, got[v])
-    first = (codes >> 6) & (BRICK - 1)
-    last = first + (codes & 63)
     steps = BRICK // SUBS
-    cells = [steps * iota((SUBS, LANES), 0) + k for k in range(steps)]
-    inside = [(c >= first) & (c < last) for c in cells]
-    dens = [jnp.where(m, x, 0.0) for m, x in zip(inside, got[:steps])]
-    return front_to_back(dens, got[steps:])
+    return front_to_back(sampled(codes, got[:steps]), got[steps:])
 
 
 def look_up(resp_ref, near, at, blocks, width, owner_ref, rank_ref, left_ref, out_refs):
@@ -355,13 +364,15 @@
         g, turn = step // n_level, lax.rem(step, n_level)
         first = row == 0
         u = jnp.maximum(jnp.where(first, g - 1, g - 2), 0)
-        far = 2 * (1 + lax.rem(row + u // 2, n_rows - 1)) + lax.rem(u + column_in, 2)
+        down = jnp.maximum(n_rows - 2 - u // 2, 0)
+        far = 2 * (1 + jnp.where(row == 1, down, lax.rem(row + u // 2, n_rows - 1))) + lax.rem(u + 1 + column_in, 2)
         head = jnp.where(first, g < 1, g < 2)
         group = jnp.where(head, jnp.where(first, 1 - column_in, g), far)
         group = jnp.where((row > 0) & (g == n_morton - 2), 2 * row + 1 - column_in, group)
         i = t - (n_dev - n_level + 2)
         beside = lax.rem(jnp.where(lax.rem(i, 2) == 0, level, partner) + 2 * (i // 2 + 1), n_level)
-        away = group * n_level + wrap(level + turn, n_level)
+        same = jnp.where(lax.rem(turn, 2) == 0, level, partner)
+        away = group * n_level + lax.rem(same + n_level - 2 * (turn // 2 + 1), n_level)
         far_or_beside = jnp.where(i >= 0, morton * n_level + beside, away)
         return jnp.where(t == 0, me, jnp.where(t == 1, morton * n_level + partner, far_or_beside))
 
@@ -388,7 +399,17 @@
 
         lax.fori_loop(low, high, body, 0)
 
-    others(lambda m, l: pl.semaphore_signal(barrier, inc=1, device_id=(m, l), device_id_type=mesh_ids))
+    def greet(m, _):
+        for k in range(n_level):
+            there = wrap(level + k, n_level)
+
+            def one():
+                pl.semaphore_signal(barrier, inc=1, device_id=(m, there), device_id_type=mesh_ids)
+
+            one() if k else pl.when(m != morton)(one)
+        return 0
+
+    lax.fori_loop(0, n_morton, greet, 0)
     for copy in copies[9:]:
         copy.start()
     for copy in copies[:9]:
@@ -420,7 +441,7 @@
 
     pl.semaphore_wait(barrier, n_dev - 1)
     others(lambda m, l: ask((m, l), me).start())
-    code_ref[me] = msg_ref[me]
+    pltpu.make_async_copy(msg_ref.at[me], code_ref.at[me], ask_recv.at[me]).start()
     for copy in copies[9:]:
         copy.wait()
     fd_ref, fe_ref, cd_ref, ce_ref = table_refs
@@ -454,20 +475,13 @@
     def two_sources(j, state):
         older, old, last, now, later = state
 
-        @pl.when(j > 0)
-        def _():
-            await_ask(now)
-
         @pl.when(j > 1)
         def _():
             start_tell(older)
-
+            start_tell(old)
+
+        await_ask(now)
         await_ask(later)
-
-        @pl.when(j > 1)
-        def _():
-            start_tell(old)
-
         fetch_source(now, even)
         march_source(last, odd)
         fetch_source(later, odd)

time: 32.3 us -> 31 us (0.960); the launches traced: 31.7 us -> 30.8 us
  Pallas kernels: 29.8 us -> 28.9 us
    pallas_call x1, Pallas kernels: 29.8 us -> 28.9 us  [shards(): pl.pallas_call(functools.partial(frame_kernel, n_morton, n_level, cap_f,...]
where the time goes in v5:
time: 31 us; the launch traced here: 30.8 us
  Pallas kernels  28.9 us (93%)
  local copies, waits for them, and re-layouts  1.24 us (4%)
  between operations  0.64 us (2%)
    pallas_call x1, Pallas kernels, shards(): pl.pallas_call(functools.partial(frame_kernel, n_morton, n_level, cap_f,...  28.9 us
    another operation x1, local copies, waits for them, and re-layouts, shards(): return (image[0].reshape(-1), image[1].reshape(-1))  1.24 us

profile of v5, /device:TPU:0, one launch (start us, length us, event | category | flops | bytes accessed | tf_op | source)
XLA Modules:
  0.0 30.8 jit_solution(18352697501581114837)
XLA Ops:
  0.6 28.9 %shard_map.140 = f32[2,2,128]{2,1,0:T(2,128)} custom-call(s32[64,128]{1,0:T(8,128)} %bitcast.13, s32[64,128]{1,0:T(8,128)} %bitcast.14, s32[64,128]{1,0:T(8,128)} %bitcast.15, s32[64,128]{1,0:T(8,128)} %bitcast.16, s32[64,128]{1,0:T(8,128)} %bitcast.17, s32[8,128]{1,0:T(8,128)} %bitcast.18, s32[8,128]{1,0:T(8,128)} %bitcast.19, s32[8,128]{1,0:T(8,128)} %bitcast.20, ...), custom_call_target="tpu_custom_call" | custom-call | tf_op jit(solution)/shard_map/pallas_call | solution.py:578
  29.6 1.2 %slice_bitcast_fusion = (f32[256]{0:T(256)}, f32[256]{0:T(256)}) fusion(f32[2,2,128]{2,1,0:T(2,128)} %shard_map.140), kind=kLoop, calls=%fused_computation | loop fusion | bytes 4096 | tf_op jit(solution)/shard_map/reshape;squeeze | solution.py:608

commit v6 on v5

--- a/solution.py
+++ b/solution.py
@@ -190,45 +190,45 @@
     return front_to_back(sampled(codes, got[:steps]), got[steps:])
 
 
-def look_up(resp_ref, near, at, blocks, width, owner_ref, rank_ref, left_ref, out_refs):
+def look_up(resp_ref, low, at, blocks, width, owner_ref, rank_ref, left_ref, out_refs):
     half = resp_ref.shape[1] // 2
-    owners = resp_ref.shape[0] - near
+    owners = resp_ref.shape[0] - low
     high = blocks // width
     cells = high * owners
     for v in range(2):
         for h in range(high):
             for w in range(width):
-                full = resp_ref[near:, v * half + at + h * width + w, :]
+                full = resp_ref[low:, v * half + at + h * width + w, :]
                 for i, piece in enumerate(split(full, 2)):
                     top = (2 * v + i) * cells + h * owners
                     left_ref[top : top + owners, w * LANES : (w + 1) * LANES] = piece
-    rows = owner_ref.shape[0]
     chunk = SUBS
     left = left_ref[: 4 * cells, : width * LANES]
-    for r in range(0, rows, chunk):
+    for r in range(0, owner_ref.shape[0], chunk):
         owner, rank = across(owner_ref, r, chunk), across(rank_ref, r, chunk)
         got = dot_nn(left, onehot(rank & (width * LANES - 1), width * LANES))
-        cell = jnp.where(owner >= near, owner - near + rank // (width * LANES) * owners, -1)
+        cell = jnp.where(owner >= low, owner - low + rank // (width * LANES) * owners, -1)
         here = iota((cells, chunk * LANES), 0) == cell
         for v in range(2):
             total = got[2 * v * cells : (2 * v + 1) * cells] + got[(2 * v + 1) * cells : (2 * v + 2) * cells]
             value = jnp.sum(jnp.where(here, total, 0.0), axis=0, keepdims=True)
             for j in range(chunk):
-                out_refs[v][r + j : r + j + 1, :] = value[:, j * LANES : (j + 1) * LANES]
-
-
-def look_near(resp_ref, near, at, blocks, owner_ref, rank_ref, out_refs):
+                out_refs[v][r + j : r + j + 1, :] += value[:, j * LANES : (j + 1) * LANES]
+
+
+def look_near(resp_ref, low, owners, at, blocks, owner_ref, rank_ref, out_refs):
     half = resp_ref.shape[1] // 2
     for r in range(0, owner_ref.shape[0], SUBS):
         rank = rank_ref[r : r + SUBS, :]
-        cell = owner_ref[r : r + SUBS, :] * blocks + rank // LANES
+        cell = (owner_ref[r : r + SUBS, :] - low) * blocks + rank // LANES
         lane = rank & (LANES - 1)
         values = [ref[r : r + SUBS, :] for ref in out_refs]
-        for d in range(near):
+        for d in range(owners):
             for b in range(blocks):
                 here = cell == d * blocks + b
                 for v in range(2):
-                    row = resp_ref[d, v * half + at + b : v * half + at + b + 1, :]
+                    top = v * half + at + b
+                    row = resp_ref[low + d, top : top + 1, :]
                     value = lanes_at(jnp.broadcast_to(row, (SUBS, LANES)), lane)
                     values[v] = jnp.where(here, value, values[v])
         for ref, value in zip(out_refs, values):
@@ -296,7 +296,7 @@
         in_sems,
         *refs,
     ) = refs
-    even, odd = refs
+    bufs = refs
     n_dev = n_morton * n_level
     nf, nc = cap_f // LANES, cap_c // LANES
     blocks = nf + nc
@@ -349,18 +349,19 @@
         )
 
     ordered = n_morton % 2 == 0 and n_morton >= 6 and n_level % 2 == 0
-    near = 2 * n_level if ordered else 0
+    near = 2 * n_level
     partner = level + 1 - 2 * lax.rem(level, 2)
     row, column_in = morton // 2, lax.rem(morton, 2)
+    start = row * near if ordered else 0
 
     def seen_by(d, m):
-        return wrap(d + n_dev - m // 2 * near, n_dev)
+        return wrap(d + n_dev - m // 2 * near, n_dev) if ordered else d
 
     def source(t):
         if not ordered:
             return lax.rem(me + n_dev - t, n_dev)
         n_rows = n_morton // 2
-        step = jnp.maximum(t - 2, 0)
+        step = jnp.maximum(t - n_level, 0)
         g, turn = step // n_level, lax.rem(step, n_level)
         first = row == 0
         u = jnp.maximum(jnp.where(first, g - 1, g - 2), 0)
@@ -369,11 +370,11 @@
         head = jnp.where(first, g < 1, g < 2)
         group = jnp.where(head, jnp.where(first, 1 - column_in, g), far)
         group = jnp.where((row > 0) & (g == n_morton - 2), 2 * row + 1 - column_in, group)
-        i = t - (n_dev - n_level + 2)
+        i = jnp.maximum(t - 2, 0)
         beside = lax.rem(jnp.where(lax.rem(i, 2) == 0, level, partner) + 2 * (i // 2 + 1), n_level)
         same = jnp.where(lax.rem(turn, 2) == 0, level, partner)
         away = group * n_level + lax.rem(same + n_level - 2 * (turn // 2 + 1), n_level)
-        far_or_beside = jnp.where(i >= 0, morton * n_level + beside, away)
+        far_or_beside = jnp.where(t < n_level, morton * n_level + beside, away)
         return jnp.where(t == 0, me, jnp.where(t == 1, morton * n_level + partner, far_or_beside))
 
     def join(k):
@@ -463,7 +464,7 @@
         for b in range(nf):
             put(i, b, *march(code_ref[i, b : b + 1, :], buf, b * LANES))
 
-    odd[...] = jnp.zeros(odd.shape, F32)
+    bufs[-1][...] = jnp.zeros(bufs[-1].shape, F32)
 
     def await_ask(d):
         ask((morton, level), d).wait_recv()
@@ -472,37 +473,54 @@
         there = device(d)
         tell(there, seen_by(me, there[0])).start()
 
-    def two_sources(j, state):
-        older, old, last, now, later = state
-
-        @pl.when(j > 1)
+    def march_some(now, last, last_buf):
+        for d in now:
+            await_ask(d)
+        spare = [b for b in bufs if b is not last_buf]
+        for i, d in enumerate(now):
+            buf = bufs[-1] if i == len(now) - 1 else spare[i]
+            fetch_source(d, buf)
+            march_source(now[i - 1] if i else last, spare[i - 1] if i else last_buf)
+
+    by = len(bufs)
+    first = tuple(source(i) for i in range(2))
+    march_some(first, me, bufs[-1])
+
+    def some_sources(j, state):
+        marched, last, now = state
+
+        @pl.when(j > 0)
         def _():
-            start_tell(older)
-            start_tell(old)
-
-        await_ask(now)
-        await_ask(later)
-        fetch_source(now, even)
-        march_source(last, odd)
-        fetch_source(later, odd)
-        march_source(now, even)
-        ahead = jnp.minimum(2 * j + 2, n_dev - 2)
-        return last, now, later, source(ahead), source(ahead + 1)
-
-    state = (me, me, me, me, source(1))
-    older, old, last, _, _ = lax.fori_loop(0, n_dev // 2, two_sources, state)
-    start_tell(older)
-    start_tell(old)
-    march_source(last, odd)
+            for d in marched:
+                start_tell(d)
+
+        march_some(now, last, bufs[-1])
+        ahead = jnp.minimum(by * (j + 1) + 2, n_dev - by)
+        return (last, *now[:-1]), now[-1], tuple(source(ahead + i) for i in range(by))
+
+    bodies = (n_dev - 2) // by
+    state = ((me,) * by, first[-1], tuple(source(2 + i) for i in range(by)))
+    marched, last, _ = lax.fori_loop(0, bodies, some_sources, state)
+    for d in marched:
+        start_tell(d)
+    rest = tuple(source(t) for t in range(by * bodies + 2, n_dev))
+    if rest:
+        march_some(rest, last, bufs[-1])
+        for d in (last, *rest[:-1]):
+            start_tell(d)
+        last = rest[-1]
+    march_source(last, bufs[-1])
     start_tell(last)
     mine = seen_by(me, morton)
     resp_ref[mine] = served_ref[me]
-    seen = owner_ref[...] - row * near
+    seen = owner_ref[...] - start
     owner_ref[...] = jnp.where(seen < 0, seen + n_dev, seen)
     rank = crank_ref[...]
-    seen = group_ref[...] * n_level + (rank & (n_level - 1)) - row * near
+    seen = group_ref[...] * n_level + (rank & (n_level - 1)) - start
     ccell_ref[...] = jnp.where(seen < 0, seen + n_dev, seen)
     crank_ref[...] = rank // n_level
+    for ref in (fc_ref, ftr_ref, cc_ref, ctr_ref):
+        ref[...] = jnp.zeros(ref.shape, F32)
 
     def await_tells(low, high):
         def one(v, _):
@@ -514,13 +532,26 @@
 
         lax.fori_loop(low, high, one, 0)
 
-    await_tells(near, n_dev)
     fine, coarse = (owner_ref, frank_ref), (ccell_ref, crank_ref)
-    look_up(resp_ref, near, nf, nc, min(nc, 2), *coarse, left_ref, (cc_ref, ctr_ref))
-    look_up(resp_ref, near, 0, nf, min(nf, 2), *fine, left_ref, (fc_ref, ftr_ref))
-    await_tells(0, near)
-    look_near(resp_ref, near, nf, nc, *coarse, (cc_ref, ctr_ref))
-    look_near(resp_ref, near, 0, nf, *fine, (fc_ref, ftr_ref))
+
+    def take_near(low, owners):
+        look_near(resp_ref, low, owners, nf, nc, *coarse, (cc_ref, ctr_ref))
+        look_near(resp_ref, low, owners, 0, nf, *fine, (fc_ref, ftr_ref))
+
+    past = 2 * near if ordered else 0
+    await_tells(past, n_dev)
+    if ordered:
+        own = column_in * n_level
+        await_tells(own, own + n_level)
+        take_near(own, n_level)
+    look_up(resp_ref, past, nf, nc, min(nc, 2), *coarse, left_ref, (cc_ref, ctr_ref))
+    look_up(resp_ref, past, 0, nf, min(nf, 2), *fine, left_ref, (fc_ref, ftr_ref))
+    if ordered:
+        await_tells(near, past)
+        take_near(near, near)
+        beside_own = (1 - column_in) * n_level
+        await_tells(beside_own, beside_own + n_level)
+        take_near(beside_own, n_level)
     blend(owner_ref.shape[0] // group_ref.shape[0], fc_ref, ftr_ref, cc_ref, ctr_ref, slab_ref)
     for k in range(1, n_level):
         join(k).start()
@@ -569,7 +600,6 @@
     tables = [fine_density, fine_emission, coarse_density, coarse_emission]
     t_rows, g_rows = fine_density.shape[0], coarse_density.shape[0]
     wide = max(f_rows * n_dev, c_rows * n_morton)
-    left_rows = 4 * n_dev * max(nf // min(nf, 2), nc // min(nc, 2))
 
     def like(x):
         return pltpu.VMEM(x.shape, x.dtype)
@@ -588,7 +618,7 @@
             pltpu.VMEM((wide, 2 * LANES), F32),
             pltpu.VMEM((4 * LANES, t_rows), BF16),
             pltpu.VMEM((-(-g_rows // LANES) * PER_ROW * 2 * BRICK, LANES), F32),
-            pltpu.VMEM((left_rows, 2 * LANES), BF16),
+            pltpu.VMEM((4 * n_dev * max(nf // min(nf, 2), nc // min(nc, 2)), 2 * LANES), BF16),
         ]
         + [pltpu.VMEM((f_rows, LANES), F32)] * 2
         + [pltpu.VMEM((c_rows, LANES), F32)] * 2
@@ -602,7 +632,7 @@
         ]
         + sems
         + [pltpu.SemaphoreType.DMA((13,))]
-        + [pltpu.VMEM((2 * LANES, cap_f), F32)] * 2,
+        + [pltpu.VMEM((2 * LANES, cap_f), F32)] * min(4, n_dev - 2),
         compiler_params=pltpu.CompilerParams(collective_id=0, has_side_effects=True),
     )(*ints, *tables)
     return image[0].reshape(-1), image[1].reshape(-1)

time: 31 us -> 30.6 us (0.987)
    pallas_call x1, Pallas kernels: 28.9 us -> 28.6 us  [shards(): pl.pallas_call(functools.partial(frame_kernel, n_morton, n_level, cap_f,...]
where the time goes in v6:
time: 30.6 us; the launch traced here: 30.4 us
  Pallas kernels  28.6 us (93%)
  local copies, waits for them, and re-layouts  1.24 us (4%)
  between operations  0.64 us (2%)
    pallas_call x1, Pallas kernels, shards(): pl.pallas_call(functools.partial(frame_kernel, n_morton, n_level, cap_f,...  28.6 us
    another operation x1, local copies, waits for them, and re-layouts, shards(): return (image[0].reshape(-1), image[1].reshape(-1))  1.24 us

profile of v6, /device:TPU:0, one launch (start us, length us, event | category | flops | bytes accessed | tf_op | source)
XLA Modules:
  0.0 30.4 jit_solution(11926667491807993867)
XLA Ops:
  0.6 28.6 %shard_map.140 = f32[2,2,128]{2,1,0:T(2,128)} custom-call(s32[64,128]{1,0:T(8,128)} %bitcast.13, s32[64,128]{1,0:T(8,128)} %bitcast.14, s32[64,128]{1,0:T(8,128)} %bitcast.15, s32[64,128]{1,0:T(8,128)} %bitcast.16, s32[64,128]{1,0:T(8,128)} %bitcast.17, s32[8,128]{1,0:T(8,128)} %bitcast.18, s32[8,128]{1,0:T(8,128)} %bitcast.19, s32[8,128]{1,0:T(8,128)} %bitcast.20, ...), custom_call_target="tpu_custom_call" | custom-call | tf_op jit(solution)/shard_map/pallas_call | solution.py:608
  29.2 1.2 %slice_bitcast_fusion = (f32[256]{0:T(256)}, f32[256]{0:T(256)}) fusion(f32[2,2,128]{2,1,0:T(2,128)} %shard_map.140), kind=kLoop, calls=%fused_computation | loop fusion | bytes 4096 | tf_op jit(solution)/shard_map/reshape;squeeze | solution.py:638
